TPU v7x, 32 devices: a 4x4x1 block of a 4x4x8 slice. The times are simulated.
32 devices in a mesh: dp: 1 (over z), cy: 4 (over y), cx: 8 (over x, core).
Axes of the slice: x: 4, y: 4, z: 1, core: 2. Of those that a mesh axis runs over, the one named last changes fastest.
The devices are a block of a 4x4x8 slice.
Arguments:
- q: bfloat16 [4096, 40, 128], P(('dp', 'cy', 'cx'))
- k: bfloat16 [4096, 40, 128], P(('dp', 'cy', 'cx'))
- v: bfloat16 [4096, 40, 128], P(('dp', 'cy', 'cx'))
Outputs:
- output: bfloat16 [4096, 40, 128], P(('dp', 'cy', 'cx'))
All inputs are finite; a program needn't handle non-finite values.
Results may differ from a plain program's by a relative error of at most 0.00345903.
Values are sent between devices in bfloat16 or wider.
A program may use at most 768 MiB of HBM per device.

v0:
```python
import jax
import jax.numpy as jnp
from jax import lax
from jax.sharding import PartitionSpec as P

NEG = -1.0e30


def init_state(c, value_a3, rep, hd):
    return (jnp.full((value_a3, rep, c), NEG, jnp.float32),
            jnp.zeros((value_a3, rep, c), jnp.float32),
            jnp.zeros((value_a3, rep, c, hd), jnp.float32))


def update(state, qc, kc, vc, mask, scale):
    m, l, acc = state
    s = jnp.einsum('qgrd,kgd->grqk', qc, kc, preferred_element_type=jnp.float32) * scale
    if mask is not None:
        s = jnp.where(mask, s, NEG)
    mn = jnp.maximum(m, jnp.max(s, axis=-1))
    p = jnp.exp(s - mn[..., None])
    alpha = jnp.exp(m - mn)
    l = alpha * l + jnp.sum(p, axis=-1)
    pv = jnp.einsum('grqk,kgd->grqd', p.astype(jnp.bfloat16), vc, preferred_element_type=jnp.float32)
    return (mn, l, alpha[..., None] * acc + pv)


def finish(state, c, nh, hd):
    m, l, acc = state
    o = (acc / l[..., None]).astype(jnp.bfloat16)
    return o.transpose(2, 0, 1, 3).reshape(c, nh, hd)


def solution(mesh):
    ncx = mesh.shape['cx']
    n = mesh.shape['cy'] * ncx
    axes = ('cy', 'cx')
    perm = [(i, (i + 1) % n) for i in range(n)]
    spec = P(('dp', 'cy', 'cx'))

    def local(q, k, v):
        t, nh, hd = q.shape
        value_a3 = k.shape[1]
        rep = nh // value_a3
        c = t // 2
        scale = hd ** -0.5
        r = lax.axis_index('cy') * ncx + lax.axis_index('cx')
        qa = q[:c].reshape(c, value_a3, rep, hd)
        qb = q[c:].reshape(c, value_a3, rep, hd)
        tri = jnp.arange(c)[None, :] <= jnp.arange(c)[:, None]
        sa = update(init_state(c, value_a3, rep, hd), qa, k[:c], v[:c], tri, scale)
        sb = update(init_state(c, value_a3, rep, hd), qb, k[:c], v[:c], None, scale)
        sb = update(sb, qb, k[c:], v[c:], tri, scale)
        kb = k
        vb = v
        for hop in range(1, n):
            kb = lax.ppermute(kb, axes, perm)
            vb = lax.ppermute(vb, axes, perm)
            src = (r - hop) % n
            sb = update(sb, qb, kb[:c], vb[:c], None, scale)
            lower = src < r
            qx = jnp.where(lower, qa, qb)
            kx = jnp.where(lower, kb[:c], kb[c:])
            vx = jnp.where(lower, vb[:c], vb[c:])
            sx = tuple(jnp.where(lower, a, b) for a, b in zip(sa, sb))
            sx = update(sx, qx, kx, vx, None, scale)
            sa = tuple(jnp.where(lower, a, b) for a, b in zip(sx, sa))
            sb = tuple(jnp.where(lower, b, a) for a, b in zip(sx, sb))
        return jnp.concatenate([finish(sa, c, nh, hd), finish(sb, c, nh, hd)], axis=0)

    return jax.shard_map(local, mesh=mesh, in_specs=(spec, spec, spec), out_specs=spec, check_vma=False)
```

profile of v0, /device:TPU:97, one launch (start us, length us, event | category | flops | bytes accessed | tf_op | source)
XLA Modules:
  0.0 1071.0 jit_solution(4223431530419778386)
XLA Ops:
  4.9 14.1 %collective-permute-done = bf16[128,40,128]{2,0,1:T(8,128)(2,1)S(1)} collective-permute-done((bf16[128,40,128]{2,0,1:T(8,128)(2,1)S(1)}, bf16[128,40,128]{2,0,1:T(8,128)(2,1)S(1)}, u32[]{:S(2)}, u32[]{:S(2)}) %collective-permute-start) | collective-permute-done | bytes 1310752 | tf_op jit(solution)/shard_map/ppermute | solution.py:57
  21.5 11.5 %collective-permute-done.31 = bf16[128,40,128]{2,0,1:T(8,128)(2,1)S(1)} collective-permute-done((bf16[128,40,128]{2,0,1:T(8,128)(2,1)S(1)}, bf16[128,40,128]{2,0,1:T(8,128)(2,1)S(1)}, u32[]{:S(2)}, u32[]{:S(2)}) %collective-permute-start.31) | collective-permute-done | bytes 1310752 | tf_op jit(solution)/shard_map/ppermute | solution.py:58
  35.6 11.5 %collective-permute-done.1 = bf16[128,40,128]{2,0,1:T(8,128)(2,1)S(1)} collective-permute-done((bf16[128,40,128]{2,0,1:T(8,128)(2,1)S(1)}, bf16[128,40,128]{2,0,1:T(8,128)(2,1)S(1)}, u32[]{:S(2)}, u32[]{:S(2)}) %collective-permute-start.1) | collective-permute-done | bytes 1310752 | tf_op jit(solution)/shard_map/ppermute | solution.py:57
  49.6 11.5 %collective-permute-done.32 = bf16[128,40,128]{2,0,1:T(8,128)(2,1)S(1)} collective-permute-done((bf16[128,40,128]{2,0,1:T(8,128)(2,1)S(1)}, bf16[128,40,128]{2,0,1:T(8,128)(2,1)S(1)}, u32[]{:S(2)}, u32[]{:S(2)}) %collective-permute-start.32) | collective-permute-done | bytes 1310752 | tf_op jit(solution)/shard_map/ppermute | solution.py:58
  63.7 11.5 %collective-permute-done.2 = bf16[128,40,128]{2,0,1:T(8,128)(2,1)S(1)} collective-permute-done((bf16[128,40,128]{2,0,1:T(8,128)(2,1)S(1)}, bf16[128,40,128]{2,0,1:T(8,128)(2,1)S(1)}, u32[]{:S(2)}, u32[]{:S(2)}) %collective-permute-start.2) | collective-permute-done | bytes 1310752 | tf_op jit(solution)/shard_map/ppermute | solution.py:57
  77.7 11.5 %collective-permute-done.33 = bf16[128,40,128]{2,0,1:T(8,128)(2,1)S(1)} collective-permute-done((bf16[128,40,128]{2,0,1:T(8,128)(2,1)S(1)}, bf16[128,40,128]{2,0,1:T(8,128)(2,1)S(1)}, u32[]{:S(2)}, u32[]{:S(2)}) %collective-permute-start.33) | collective-permute-done | bytes 1310752 | tf_op jit(solution)/shard_map/ppermute | solution.py:58
  91.8 11.5 %collective-permute-done.3 = bf16[128,40,128]{2,0,1:T(8,128)(2,1)S(1)} collective-permute-done((bf16[128,40,128]{2,0,1:T(8,128)(2,1)S(1)}, bf16[128,40,128]{2,0,1:T(8,128)(2,1)S(1)}, u32[]{:S(2)}, u32[]{:S(2)}) %collective-permute-start.3) | collective-permute-done | bytes 1310752 | tf_op jit(solution)/shard_map/ppermute | solution.py:57
  105.8 11.5 %collective-permute-done.34 = bf16[128,40,128]{2,0,1:T(8,128)(2,1)S(1)} collective-permute-done((bf16[128,40,128]{2,0,1:T(8,128)(2,1)S(1)}, bf16[128,40,128]{2,0,1:T(8,128)(2,1)S(1)}, u32[]{:S(2)}, u32[]{:S(2)}) %collective-permute-start.34) | collective-permute-done | bytes 1310752 | tf_op jit(solution)/shard_map/ppermute | solution.py:58
  119.9 11.5 %collective-permute-done.4 = bf16[128,40,128]{2,0,1:T(8,128)(2,1)S(1)} collective-permute-done((bf16[128,40,128]{2,0,1:T(8,128)(2,1)S(1)}, bf16[128,40,128]{2,0,1:T(8,128)(2,1)S(1)}, u32[]{:S(2)}, u32[]{:S(2)}) %collective-permute-start.4) | collective-permute-done | bytes 1310752 | tf_op jit(solution)/shard_map/ppermute | solution.py:57
  133.9 11.5 %collective-permute-done.35 = bf16[128,40,128]{2,0,1:T(8,128)(2,1)S(1)} collective-permute-done((bf16[128,40,128]{2,0,1:T(8,128)(2,1)S(1)}, bf16[128,40,128]{2,0,1:T(8,128)(2,1)S(1)}, u32[]{:S(2)}, u32[]{:S(2)}) %collective-permute-start.35) | collective-permute-done | bytes 1310752 | tf_op jit(solution)/shard_map/ppermute | solution.py:58
  147.9 11.5 %collective-permute-done.5 = bf16[128,40,128]{2,0,1:T(8,128)(2,1)S(1)} collective-permute-done((bf16[128,40,128]{2,0,1:T(8,128)(2,1)S(1)}, bf16[128,40,128]{2,0,1:T(8,128)(2,1)S(1)}, u32[]{:S(2)}, u32[]{:S(2)}) %collective-permute-start.5) | collective-permute-done | bytes 1310752 | tf_op jit(solution)/shard_map/ppermute | solution.py:57
  162.0 11.5 %collective-permute-done.36 = bf16[128,40,128]{2,0,1:T(8,128)(2,1)S(1)} collective-permute-done((bf16[128,40,128]{2,0,1:T(8,128)(2,1)S(1)}, bf16[128,40,128]{2,0,1:T(8,128)(2,1)S(1)}, u32[]{:S(2)}, u32[]{:S(2)}) %collective-permute-start.36) | collective-permute-done | bytes 1310752 | tf_op jit(solution)/shard_map/ppermute | solution.py:58
  176.0 11.5 %collective-permute-done.6 = bf16[128,40,128]{2,0,1:T(8,128)(2,1)S(1)} collective-permute-done((bf16[128,40,128]{2,0,1:T(8,128)(2,1)S(1)}, bf16[128,40,128]{2,0,1:T(8,128)(2,1)S(1)}, u32[]{:S(2)}, u32[]{:S(2)}) %collective-permute-start.6) | collective-permute-done | bytes 1310752 | tf_op jit(solution)/shard_map/ppermute | solution.py:57
  190.1 11.5 %collective-permute-done.37 = bf16[128,40,128]{2,0,1:T(8,128)(2,1)S(1)} collective-permute-done((bf16[128,40,128]{2,0,1:T(8,128)(2,1)S(1)}, bf16[128,40,128]{2,0,1:T(8,128)(2,1)S(1)}, u32[]{:S(2)}, u32[]{:S(2)}) %collective-permute-start.37) | collective-permute-done | bytes 1310752 | tf_op jit(solution)/shard_map/ppermute | solution.py:58
  204.1 11.5 %collective-permute-done.7 = bf16[128,40,128]{2,0,1:T(8,128)(2,1)S(1)} collective-permute-done((bf16[128,40,128]{2,0,1:T(8,128)(2,1)S(1)}, bf16[128,40,128]{2,0,1:T(8,128)(2,1)S(1)}, u32[]{:S(2)}, u32[]{:S(2)}) %collective-permute-start.7) | collective-permute-done | bytes 1310752 | tf_op jit(solution)/shard_map/ppermute | solution.py:57
  218.2 11.5 %collective-permute-done.38 = bf16[128,40,128]{2,0,1:T(8,128)(2,1)S(1)} collective-permute-done((bf16[128,40,128]{2,0,1:T(8,128)(2,1)S(1)}, bf16[128,40,128]{2,0,1:T(8,128)(2,1)S(1)}, u32[]{:S(2)}, u32[]{:S(2)}) %collective-permute-start.38) | collective-permute-done | bytes 1310752 | tf_op jit(solution)/shard_map/ppermute | solution.py:58
  232.2 11.5 %collective-permute-done.8 = bf16[128,40,128]{2,0,1:T(8,128)(2,1)S(1)} collective-permute-done((bf16[128,40,128]{2,0,1:T(8,128)(2,1)S(1)}, bf16[128,40,128]{2,0,1:T(8,128)(2,1)S(1)}, u32[]{:S(2)}, u32[]{:S(2)}) %collective-permute-start.8) | collective-permute-done | bytes 1310752 | tf_op jit(solution)/shard_map/ppermute | solution.py:57
  246.3 11.5 %collective-permute-done.39 = bf16[128,40,128]{2,0,1:T(8,128)(2,1)S(1)} collective-permute-done((bf16[128,40,128]{2,0,1:T(8,128)(2,1)S(1)}, bf16[128,40,128]{2,0,1:T(8,128)(2,1)S(1)}, u32[]{:S(2)}, u32[]{:S(2)}) %collective-permute-start.39) | collective-permute-done | bytes 1310752 | tf_op jit(solution)/shard_map/ppermute | solution.py:58
  260.3 11.5 %collective-permute-done.9 = bf16[128,40,128]{2,0,1:T(8,128)(2,1)S(1)} collective-permute-done((bf16[128,40,128]{2,0,1:T(8,128)(2,1)S(1)}, bf16[128,40,128]{2,0,1:T(8,128)(2,1)S(1)}, u32[]{:S(2)}, u32[]{:S(2)}) %collective-permute-start.9) | collective-permute-done | bytes 1310752 | tf_op jit(solution)/shard_map/ppermute | solution.py:57
  274.4 11.5 %collective-permute-done.40 = bf16[128,40,128]{2,0,1:T(8,128)(2,1)S(1)} collective-permute-done((bf16[128,40,128]{2,0,1:T(8,128)(2,1)S(1)}, bf16[128,40,128]{2,0,1:T(8,128)(2,1)S(1)}, u32[]{:S(2)}, u32[]{:S(2)}) %collective-permute-start.40) | collective-permute-done | bytes 1310752 | tf_op jit(solution)/shard_map/ppermute | solution.py:58
  288.4 11.5 %collective-permute-done.10 = bf16[128,40,128]{2,0,1:T(8,128)(2,1)S(1)} collective-permute-done((bf16[128,40,128]{2,0,1:T(8,128)(2,1)S(1)}, bf16[128,40,128]{2,0,1:T(8,128)(2,1)S(1)}, u32[]{:S(2)}, u32[]{:S(2)}) %collective-permute-start.10) | collective-permute-done | bytes 1310752 | tf_op jit(solution)/shard_map/ppermute | solution.py:57
  302.4 11.5 %collective-permute-done.41 = bf16[128,40,128]{2,0,1:T(8,128)(2,1)S(1)} collective-permute-done((bf16[128,40,128]{2,0,1:T(8,128)(2,1)S(1)}, bf16[128,40,128]{2,0,1:T(8,128)(2,1)S(1)}, u32[]{:S(2)}, u32[]{:S(2)}) %collective-permute-start.41) | collective-permute-done | bytes 1310752 | tf_op jit(solution)/shard_map/ppermute | solution.py:58
  316.5 11.5 %collective-permute-done.11 = bf16[128,40,128]{2,0,1:T(8,128)(2,1)S(1)} collective-permute-done((bf16[128,40,128]{2,0,1:T(8,128)(2,1)S(1)}, bf16[128,40,128]{2,0,1:T(8,128)(2,1)S(1)}, u32[]{:S(2)}, u32[]{:S(2)}) %collective-permute-start.11) | collective-permute-done | bytes 1310752 | tf_op jit(solution)/shard_map/ppermute | solution.py:57
  330.5 11.5 %collective-permute-done.42 = bf16[128,40,128]{2,0,1:T(8,128)(2,1)S(1)} collective-permute-done((bf16[128,40,128]{2,0,1:T(8,128)(2,1)S(1)}, bf16[128,40,128]{2,0,1:T(8,128)(2,1)S(1)}, u32[]{:S(2)}, u32[]{:S(2)}) %collective-permute-start.42) | collective-permute-done | bytes 1310752 | tf_op jit(solution)/shard_map/ppermute | solution.py:58
  344.6 11.5 %collective-permute-done.12 = bf16[128,40,128]{2,0,1:T(8,128)(2,1)S(1)} collective-permute-done((bf16[128,40,128]{2,0,1:T(8,128)(2,1)S(1)}, bf16[128,40,128]{2,0,1:T(8,128)(2,1)S(1)}, u32[]{:S(2)}, u32[]{:S(2)}) %collective-permute-start.12) | collective-permute-done | bytes 1310752 | tf_op jit(solution)/shard_map/ppermute | solution.py:57
  358.6 11.5 %collective-permute-done.43 = bf16[128,40,128]{2,0,1:T(8,128)(2,1)S(1)} collective-permute-done((bf16[128,40,128]{2,0,1:T(8,128)(2,1)S(1)}, bf16[128,40,128]{2,0,1:T(8,128)(2,1)S(1)}, u32[]{:S(2)}, u32[]{:S(2)}) %collective-permute-start.43) | collective-permute-done | bytes 1310752 | tf_op jit(solution)/shard_map/ppermute | solution.py:58
  372.7 11.5 %collective-permute-done.13 = bf16[128,40,128]{2,0,1:T(8,128)(2,1)S(1)} collective-permute-done((bf16[128,40,128]{2,0,1:T(8,128)(2,1)S(1)}, bf16[128,40,128]{2,0,1:T(8,128)(2,1)S(1)}, u32[]{:S(2)}, u32[]{:S(2)}) %collective-permute-start.13) | collective-permute-done | bytes 1310752 | tf_op jit(solution)/shard_map/ppermute | solution.py:57
  386.7 11.5 %collective-permute-done.44 = bf16[128,40,128]{2,0,1:T(8,128)(2,1)S(1)} collective-permute-done((bf16[128,40,128]{2,0,1:T(8,128)(2,1)S(1)}, bf16[128,40,128]{2,0,1:T(8,128)(2,1)S(1)}, u32[]{:S(2)}, u32[]{:S(2)}) %collective-permute-start.44) | collective-permute-done | bytes 1310752 | tf_op jit(solution)/shard_map/ppermute | solution.py:58
  400.8 11.5 %collective-permute-done.14 = bf16[128,40,128]{2,0,1:T(8,128)(2,1)S(1)} collective-permute-done((bf16[128,40,128]{2,0,1:T(8,128)(2,1)S(1)}, bf16[128,40,128]{2,0,1:T(8,128)(2,1)S(1)}, u32[]{:S(2)}, u32[]{:S(2)}) %collective-permute-start.14) | collective-permute-done | bytes 1310752 | tf_op jit(solution)/shard_map/ppermute | solution.py:57
  414.8 11.5 %collective-permute-done.45 = bf16[128,40,128]{2,0,1:T(8,128)(2,1)S(1)} collective-permute-done((bf16[128,40,128]{2,0,1:T(8,128)(2,1)S(1)}, bf16[128,40,128]{2,0,1:T(8,128)(2,1)S(1)}, u32[]{:S(2)}, u32[]{:S(2)}) %collective-permute-start.45) | collective-permute-done | bytes 1310752 | tf_op jit(solution)/shard_map/ppermute | solution.py:58
  428.8 11.5 %collective-permute-done.15 = bf16[128,40,128]{2,0,1:T(8,128)(2,1)S(1)} collective-permute-done((bf16[128,40,128]{2,0,1:T(8,128)(2,1)S(1)}, bf16[128,40,128]{2,0,1:T(8,128)(2,1)S(1)}, u32[]{:S(2)}, u32[]{:S(2)}) %collective-permute-start.15) | collective-permute-done | bytes 1310752 | tf_op jit(solution)/shard_map/ppermute | solution.py:57
  442.9 11.5 %collective-permute-done.46 = bf16[128,40,128]{2,0,1:T(8,128)(2,1)S(1)} collective-permute-done((bf16[128,40,128]{2,0,1:T(8,128)(2,1)S(1)}, bf16[128,40,128]{2,0,1:T(8,128)(2,1)S(1)}, u32[]{:S(2)}, u32[]{:S(2)}) %collective-permute-start.46) | collective-permute-done | bytes 1310752 | tf_op jit(solution)/shard_map/ppermute | solution.py:58
  456.9 11.5 %collective-permute-done.16 = bf16[128,40,128]{2,0,1:T(8,128)(2,1)S(1)} collective-permute-done((bf16[128,40,128]{2,0,1:T(8,128)(2,1)S(1)}, bf16[128,40,128]{2,0,1:T(8,128)(2,1)S(1)}, u32[]{:S(2)}, u32[]{:S(2)}) %collective-permute-start.16) | collective-permute-done | bytes 1310752 | tf_op jit(solution)/shard_map/ppermute | solution.py:57
  471.0 11.5 %collective-permute-done.47 = bf16[128,40,128]{2,0,1:T(8,128)(2,1)S(1)} collective-permute-done((bf16[128,40,128]{2,0,1:T(8,128)(2,1)S(1)}, bf16[128,40,128]{2,0,1:T(8,128)(2,1)S(1)}, u32[]{:S(2)}, u32[]{:S(2)}) %collective-permute-start.47) | collective-permute-done | bytes 1310752 | tf_op jit(solution)/shard_map/ppermute | solution.py:58
  485.0 11.5 %collective-permute-done.17 = bf16[128,40,128]{2,0,1:T(8,128)(2,1)S(1)} collective-permute-done((bf16[128,40,128]{2,0,1:T(8,128)(2,1)S(1)}, bf16[128,40,128]{2,0,1:T(8,128)(2,1)S(1)}, u32[]{:S(2)}, u32[]{:S(2)}) %collective-permute-start.17) | collective-permute-done | bytes 1310752 | tf_op jit(solution)/shard_map/ppermute | solution.py:57
  499.1 11.5 %collective-permute-done.48 = bf16[128,40,128]{2,0,1:T(8,128)(2,1)S(1)} collective-permute-done((bf16[128,40,128]{2,0,1:T(8,128)(2,1)S(1)}, bf16[128,40,128]{2,0,1:T(8,128)(2,1)S(1)}, u32[]{:S(2)}, u32[]{:S(2)}) %collective-permute-start.48) | collective-permute-done | bytes 1310752 | tf_op jit(solution)/shard_map/ppermute | solution.py:58
  513.1 11.5 %collective-permute-done.18 = bf16[128,40,128]{2,0,1:T(8,128)(2,1)S(1)} collective-permute-done((bf16[128,40,128]{2,0,1:T(8,128)(2,1)S(1)}, bf16[128,40,128]{2,0,1:T(8,128)(2,1)S(1)}, u32[]{:S(2)}, u32[]{:S(2)}) %collective-permute-start.18) | collective-permute-done | bytes 1310752 | tf_op jit(solution)/shard_map/ppermute | solution.py:57
  527.2 11.5 %collective-permute-done.49 = bf16[128,40,128]{2,0,1:T(8,128)(2,1)S(1)} collective-permute-done((bf16[128,40,128]{2,0,1:T(8,128)(2,1)S(1)}, bf16[128,40,128]{2,0,1:T(8,128)(2,1)S(1)}, u32[]{:S(2)}, u32[]{:S(2)}) %collective-permute-start.49) | collective-permute-done | bytes 1310752 | tf_op jit(solution)/shard_map/ppermute | solution.py:58
  542.0 10.7 collective-permute-done.19
  557.2 9.6 collective-permute-done.50
  600.2 8.7 collective-permute-done.21
  628.2 8.8 collective-permute-done.22
  656.2 8.9 collective-permute-done.23
  684.4 8.8 collective-permute-done.24
  712.4 8.9 collective-permute-done.25
  740.5 8.9 collective-permute-done.26
  796.8 8.7 collective-permute-done.28
  824.8 8.8 collective-permute-done.29
  (920 shorter events, 534.4 us)
Async XLA Ops:
  4.8 28.3 %collective-permute-start.31 = (bf16[128,40,128]{2,0,1:T(8,128)(2,1)S(1)}, bf16[128,40,128]{2,0,1:T(8,128)(2,1)S(1)}, u32[]{:S(2)}, u32[]{:S(2)}) collective-permute-start(bf16[128,40,128]{2,0,1:T(8,128)(2,1)S(1)} %copy.9), channel_id=1, source_target_pairs={{0,1},{1,2},{2,3},{3,4},{4,5},{5,6},{6,7},{7,8},{8,9},{9,10},{10,1... | collective-permute-start | bytes 3932168 | tf_op jit(solution)/shard_map/ppermute | solution.py:58
  19.0 28.1 %collective-permute-start.1 = (bf16[128,40,128]{2,0,1:T(8,128)(2,1)S(1)}, bf16[128,40,128]{2,0,1:T(8,128)(2,1)S(1)}, u32[]{:S(2)}, u32[]{:S(2)}) collective-permute-start(bf16[128,40,128]{2,0,1:T(8,128)(2,1)S(1)} %collective-permute-done), channel_id=1, source_target_pairs={{0,1},{1,2},{2,3},{3,4},{4,5},{5,6},{6,7},{7,8},{8,9},{9,10},{10,1... | collective-permute-start | bytes 3932168 | tf_op jit(solution)/shard_map/ppermute | solution.py:57
  33.1 28.1 %collective-permute-start.32 = (bf16[128,40,128]{2,0,1:T(8,128)(2,1)S(1)}, bf16[128,40,128]{2,0,1:T(8,128)(2,1)S(1)}, u32[]{:S(2)}, u32[]{:S(2)}) collective-permute-start(bf16[128,40,128]{2,0,1:T(8,128)(2,1)S(1)} %collective-permute-done.31), channel_id=1, source_target_pairs={{0,1},{1,2},{2,3},{3,4},{4,5},{5,6},{6,7},{7,8},{8,9},{9,10},{10,1... | collective-permute-start | bytes 3932168 | tf_op jit(solution)/shard_map/ppermute | solution.py:58
  47.1 28.1 %collective-permute-start.2 = (bf16[128,40,128]{2,0,1:T(8,128)(2,1)S(1)}, bf16[128,40,128]{2,0,1:T(8,128)(2,1)S(1)}, u32[]{:S(2)}, u32[]{:S(2)}) collective-permute-start(bf16[128,40,128]{2,0,1:T(8,128)(2,1)S(1)} %collective-permute-done.1), channel_id=1, source_target_pairs={{0,1},{1,2},{2,3},{3,4},{4,5},{5,6},{6,7},{7,8},{8,9},{9,10},{10,1... | collective-permute-start | bytes 3932168 | tf_op jit(solution)/shard_map/ppermute | solution.py:57
  61.2 28.1 %collective-permute-start.33 = (bf16[128,40,128]{2,0,1:T(8,128)(2,1)S(1)}, bf16[128,40,128]{2,0,1:T(8,128)(2,1)S(1)}, u32[]{:S(2)}, u32[]{:S(2)}) collective-permute-start(bf16[128,40,128]{2,0,1:T(8,128)(2,1)S(1)} %collective-permute-done.32), channel_id=1, source_target_pairs={{0,1},{1,2},{2,3},{3,4},{4,5},{5,6},{6,7},{7,8},{8,9},{9,10},{10,1... | collective-permute-start | bytes 3932168 | tf_op jit(solution)/shard_map/ppermute | solution.py:58
  75.2 28.1 %collective-permute-start.3 = (bf16[128,40,128]{2,0,1:T(8,128)(2,1)S(1)}, bf16[128,40,128]{2,0,1:T(8,128)(2,1)S(1)}, u32[]{:S(2)}, u32[]{:S(2)}) collective-permute-start(bf16[128,40,128]{2,0,1:T(8,128)(2,1)S(1)} %collective-permute-done.2), channel_id=1, source_target_pairs={{0,1},{1,2},{2,3},{3,4},{4,5},{5,6},{6,7},{7,8},{8,9},{9,10},{10,1... | collective-permute-start | bytes 3932168 | tf_op jit(solution)/shard_map/ppermute | solution.py:57
  89.3 28.1 %collective-permute-start.34 = (bf16[128,40,128]{2,0,1:T(8,128)(2,1)S(1)}, bf16[128,40,128]{2,0,1:T(8,128)(2,1)S(1)}, u32[]{:S(2)}, u32[]{:S(2)}) collective-permute-start(bf16[128,40,128]{2,0,1:T(8,128)(2,1)S(1)} %collective-permute-done.33), channel_id=1, source_target_pairs={{0,1},{1,2},{2,3},{3,4},{4,5},{5,6},{6,7},{7,8},{8,9},{9,10},{10,1... | collective-permute-start | bytes 3932168 | tf_op jit(solution)/shard_map/ppermute | solution.py:58
  103.3 28.1 %collective-permute-start.4 = (bf16[128,40,128]{2,0,1:T(8,128)(2,1)S(1)}, bf16[128,40,128]{2,0,1:T(8,128)(2,1)S(1)}, u32[]{:S(2)}, u32[]{:S(2)}) collective-permute-start(bf16[128,40,128]{2,0,1:T(8,128)(2,1)S(1)} %collective-permute-done.3), channel_id=1, source_target_pairs={{0,1},{1,2},{2,3},{3,4},{4,5},{5,6},{6,7},{7,8},{8,9},{9,10},{10,1... | collective-permute-start | bytes 3932168 | tf_op jit(solution)/shard_map/ppermute | solution.py:57
  117.4 28.1 %collective-permute-start.35 = (bf16[128,40,128]{2,0,1:T(8,128)(2,1)S(1)}, bf16[128,40,128]{2,0,1:T(8,128)(2,1)S(1)}, u32[]{:S(2)}, u32[]{:S(2)}) collective-permute-start(bf16[128,40,128]{2,0,1:T(8,128)(2,1)S(1)} %collective-permute-done.34), channel_id=1, source_target_pairs={{0,1},{1,2},{2,3},{3,4},{4,5},{5,6},{6,7},{7,8},{8,9},{9,10},{10,1... | collective-permute-start | bytes 3932168 | tf_op jit(solution)/shard_map/ppermute | solution.py:58
  131.4 28.1 %collective-permute-start.5 = (bf16[128,40,128]{2,0,1:T(8,128)(2,1)S(1)}, bf16[128,40,128]{2,0,1:T(8,128)(2,1)S(1)}, u32[]{:S(2)}, u32[]{:S(2)}) collective-permute-start(bf16[128,40,128]{2,0,1:T(8,128)(2,1)S(1)} %collective-permute-done.4), channel_id=1, source_target_pairs={{0,1},{1,2},{2,3},{3,4},{4,5},{5,6},{6,7},{7,8},{8,9},{9,10},{10,1... | collective-permute-start | bytes 3932168 | tf_op jit(solution)/shard_map/ppermute | solution.py:57
  145.4 28.1 %collective-permute-start.36 = (bf16[128,40,128]{2,0,1:T(8,128)(2,1)S(1)}, bf16[128,40,128]{2,0,1:T(8,128)(2,1)S(1)}, u32[]{:S(2)}, u32[]{:S(2)}) collective-permute-start(bf16[128,40,128]{2,0,1:T(8,128)(2,1)S(1)} %collective-permute-done.35), channel_id=1, source_target_pairs={{0,1},{1,2},{2,3},{3,4},{4,5},{5,6},{6,7},{7,8},{8,9},{9,10},{10,1... | collective-permute-start | bytes 3932168 | tf_op jit(solution)/shard_map/ppermute | solution.py:58
  159.5 28.1 %collective-permute-start.6 = (bf16[128,40,128]{2,0,1:T(8,128)(2,1)S(1)}, bf16[128,40,128]{2,0,1:T(8,128)(2,1)S(1)}, u32[]{:S(2)}, u32[]{:S(2)}) collective-permute-start(bf16[128,40,128]{2,0,1:T(8,128)(2,1)S(1)} %collective-permute-done.5), channel_id=1, source_target_pairs={{0,1},{1,2},{2,3},{3,4},{4,5},{5,6},{6,7},{7,8},{8,9},{9,10},{10,1... | collective-permute-start | bytes 3932168 | tf_op jit(solution)/shard_map/ppermute | solution.py:57
  173.5 28.1 %collective-permute-start.37 = (bf16[128,40,128]{2,0,1:T(8,128)(2,1)S(1)}, bf16[128,40,128]{2,0,1:T(8,128)(2,1)S(1)}, u32[]{:S(2)}, u32[]{:S(2)}) collective-permute-start(bf16[128,40,128]{2,0,1:T(8,128)(2,1)S(1)} %collective-permute-done.36), channel_id=1, source_target_pairs={{0,1},{1,2},{2,3},{3,4},{4,5},{5,6},{6,7},{7,8},{8,9},{9,10},{10,1... | collective-permute-start | bytes 3932168 | tf_op jit(solution)/shard_map/ppermute | solution.py:58
  187.6 28.1 %collective-permute-start.7 = (bf16[128,40,128]{2,0,1:T(8,128)(2,1)S(1)}, bf16[128,40,128]{2,0,1:T(8,128)(2,1)S(1)}, u32[]{:S(2)}, u32[]{:S(2)}) collective-permute-start(bf16[128,40,128]{2,0,1:T(8,128)(2,1)S(1)} %collective-permute-done.6), channel_id=1, source_target_pairs={{0,1},{1,2},{2,3},{3,4},{4,5},{5,6},{6,7},{7,8},{8,9},{9,10},{10,1... | collective-permute-start | bytes 3932168 | tf_op jit(solution)/shard_map/ppermute | solution.py:57
  201.6 28.1 %collective-permute-start.38 = (bf16[128,40,128]{2,0,1:T(8,128)(2,1)S(1)}, bf16[128,40,128]{2,0,1:T(8,128)(2,1)S(1)}, u32[]{:S(2)}, u32[]{:S(2)}) collective-permute-start(bf16[128,40,128]{2,0,1:T(8,128)(2,1)S(1)} %collective-permute-done.37), channel_id=1, source_target_pairs={{0,1},{1,2},{2,3},{3,4},{4,5},{5,6},{6,7},{7,8},{8,9},{9,10},{10,1... | collective-permute-start | bytes 3932168 | tf_op jit(solution)/shard_map/ppermute | solution.py:58
  215.7 28.1 %collective-permute-start.8 = (bf16[128,40,128]{2,0,1:T(8,128)(2,1)S(1)}, bf16[128,40,128]{2,0,1:T(8,128)(2,1)S(1)}, u32[]{:S(2)}, u32[]{:S(2)}) collective-permute-start(bf16[128,40,128]{2,0,1:T(8,128)(2,1)S(1)} %collective-permute-done.7), channel_id=1, source_target_pairs={{0,1},{1,2},{2,3},{3,4},{4,5},{5,6},{6,7},{7,8},{8,9},{9,10},{10,1... | collective-permute-start | bytes 3932168 | tf_op jit(solution)/shard_map/ppermute | solution.py:57
  229.7 28.1 %collective-permute-start.39 = (bf16[128,40,128]{2,0,1:T(8,128)(2,1)S(1)}, bf16[128,40,128]{2,0,1:T(8,128)(2,1)S(1)}, u32[]{:S(2)}, u32[]{:S(2)}) collective-permute-start(bf16[128,40,128]{2,0,1:T(8,128)(2,1)S(1)} %collective-permute-done.38), channel_id=1, source_target_pairs={{0,1},{1,2},{2,3},{3,4},{4,5},{5,6},{6,7},{7,8},{8,9},{9,10},{10,1... | collective-permute-start | bytes 3932168 | tf_op jit(solution)/shard_map/ppermute | solution.py:58
  243.8 28.1 %collective-permute-start.9 = (bf16[128,40,128]{2,0,1:T(8,128)(2,1)S(1)}, bf16[128,40,128]{2,0,1:T(8,128)(2,1)S(1)}, u32[]{:S(2)}, u32[]{:S(2)}) collective-permute-start(bf16[128,40,128]{2,0,1:T(8,128)(2,1)S(1)} %collective-permute-done.8), channel_id=1, source_target_pairs={{0,1},{1,2},{2,3},{3,4},{4,5},{5,6},{6,7},{7,8},{8,9},{9,10},{10,1... | collective-permute-start | bytes 3932168 | tf_op jit(solution)/shard_map/ppermute | solution.py:57
  257.8 28.1 %collective-permute-start.40 = (bf16[128,40,128]{2,0,1:T(8,128)(2,1)S(1)}, bf16[128,40,128]{2,0,1:T(8,128)(2,1)S(1)}, u32[]{:S(2)}, u32[]{:S(2)}) collective-permute-start(bf16[128,40,128]{2,0,1:T(8,128)(2,1)S(1)} %collective-permute-done.39), channel_id=1, source_target_pairs={{0,1},{1,2},{2,3},{3,4},{4,5},{5,6},{6,7},{7,8},{8,9},{9,10},{10,1... | collective-permute-start | bytes 3932168 | tf_op jit(solution)/shard_map/ppermute | solution.py:58
  271.8 28.1 %collective-permute-start.10 = (bf16[128,40,128]{2,0,1:T(8,128)(2,1)S(1)}, bf16[128,40,128]{2,0,1:T(8,128)(2,1)S(1)}, u32[]{:S(2)}, u32[]{:S(2)}) collective-permute-start(bf16[128,40,128]{2,0,1:T(8,128)(2,1)S(1)} %collective-permute-done.9), channel_id=1, source_target_pairs={{0,1},{1,2},{2,3},{3,4},{4,5},{5,6},{6,7},{7,8},{8,9},{9,10},{10,1... | collective-permute-start | bytes 3932168 | tf_op jit(solution)/shard_map/ppermute | solution.py:57
  285.9 28.1 %collective-permute-start.41 = (bf16[128,40,128]{2,0,1:T(8,128)(2,1)S(1)}, bf16[128,40,128]{2,0,1:T(8,128)(2,1)S(1)}, u32[]{:S(2)}, u32[]{:S(2)}) collective-permute-start(bf16[128,40,128]{2,0,1:T(8,128)(2,1)S(1)} %collective-permute-done.40), channel_id=1, source_target_pairs={{0,1},{1,2},{2,3},{3,4},{4,5},{5,6},{6,7},{7,8},{8,9},{9,10},{10,1... | collective-permute-start | bytes 3932168 | tf_op jit(solution)/shard_map/ppermute | solution.py:58
  299.9 28.1 %collective-permute-start.11 = (bf16[128,40,128]{2,0,1:T(8,128)(2,1)S(1)}, bf16[128,40,128]{2,0,1:T(8,128)(2,1)S(1)}, u32[]{:S(2)}, u32[]{:S(2)}) collective-permute-start(bf16[128,40,128]{2,0,1:T(8,128)(2,1)S(1)} %collective-permute-done.10), channel_id=1, source_target_pairs={{0,1},{1,2},{2,3},{3,4},{4,5},{5,6},{6,7},{7,8},{8,9},{9,10},{10,1... | collective-permute-start | bytes 3932168 | tf_op jit(solution)/shard_map/ppermute | solution.py:57
  314.0 28.1 %collective-permute-start.42 = (bf16[128,40,128]{2,0,1:T(8,128)(2,1)S(1)}, bf16[128,40,128]{2,0,1:T(8,128)(2,1)S(1)}, u32[]{:S(2)}, u32[]{:S(2)}) collective-permute-start(bf16[128,40,128]{2,0,1:T(8,128)(2,1)S(1)} %collective-permute-done.41), channel_id=1, source_target_pairs={{0,1},{1,2},{2,3},{3,4},{4,5},{5,6},{6,7},{7,8},{8,9},{9,10},{10,1... | collective-permute-start | bytes 3932168 | tf_op jit(solution)/shard_map/ppermute | solution.py:58
  328.0 28.1 %collective-permute-start.12 = (bf16[128,40,128]{2,0,1:T(8,128)(2,1)S(1)}, bf16[128,40,128]{2,0,1:T(8,128)(2,1)S(1)}, u32[]{:S(2)}, u32[]{:S(2)}) collective-permute-start(bf16[128,40,128]{2,0,1:T(8,128)(2,1)S(1)} %collective-permute-done.11), channel_id=1, source_target_pairs={{0,1},{1,2},{2,3},{3,4},{4,5},{5,6},{6,7},{7,8},{8,9},{9,10},{10,1... | collective-permute-start | bytes 3932168 | tf_op jit(solution)/shard_map/ppermute | solution.py:57
  342.1 28.1 %collective-permute-start.43 = (bf16[128,40,128]{2,0,1:T(8,128)(2,1)S(1)}, bf16[128,40,128]{2,0,1:T(8,128)(2,1)S(1)}, u32[]{:S(2)}, u32[]{:S(2)}) collective-permute-start(bf16[128,40,128]{2,0,1:T(8,128)(2,1)S(1)} %collective-permute-done.42), channel_id=1, source_target_pairs={{0,1},{1,2},{2,3},{3,4},{4,5},{5,6},{6,7},{7,8},{8,9},{9,10},{10,1... | collective-permute-start | bytes 3932168 | tf_op jit(solution)/shard_map/ppermute | solution.py:58
  356.1 28.1 %collective-permute-start.13 = (bf16[128,40,128]{2,0,1:T(8,128)(2,1)S(1)}, bf16[128,40,128]{2,0,1:T(8,128)(2,1)S(1)}, u32[]{:S(2)}, u32[]{:S(2)}) collective-permute-start(bf16[128,40,128]{2,0,1:T(8,128)(2,1)S(1)} %collective-permute-done.12), channel_id=1, source_target_pairs={{0,1},{1,2},{2,3},{3,4},{4,5},{5,6},{6,7},{7,8},{8,9},{9,10},{10,1... | collective-permute-start | bytes 3932168 | tf_op jit(solution)/shard_map/ppermute | solution.py:57
  370.2 28.1 %collective-permute-start.44 = (bf16[128,40,128]{2,0,1:T(8,128)(2,1)S(1)}, bf16[128,40,128]{2,0,1:T(8,128)(2,1)S(1)}, u32[]{:S(2)}, u32[]{:S(2)}) collective-permute-start(bf16[128,40,128]{2,0,1:T(8,128)(2,1)S(1)} %collective-permute-done.43), channel_id=1, source_target_pairs={{0,1},{1,2},{2,3},{3,4},{4,5},{5,6},{6,7},{7,8},{8,9},{9,10},{10,1... | collective-permute-start | bytes 3932168 | tf_op jit(solution)/shard_map/ppermute | solution.py:58
  384.2 28.1 %collective-permute-start.14 = (bf16[128,40,128]{2,0,1:T(8,128)(2,1)S(1)}, bf16[128,40,128]{2,0,1:T(8,128)(2,1)S(1)}, u32[]{:S(2)}, u32[]{:S(2)}) collective-permute-start(bf16[128,40,128]{2,0,1:T(8,128)(2,1)S(1)} %collective-permute-done.13), channel_id=1, source_target_pairs={{0,1},{1,2},{2,3},{3,4},{4,5},{5,6},{6,7},{7,8},{8,9},{9,10},{10,1... | collective-permute-start | bytes 3932168 | tf_op jit(solution)/shard_map/ppermute | solution.py:57
  398.3 28.1 %collective-permute-start.45 = (bf16[128,40,128]{2,0,1:T(8,128)(2,1)S(1)}, bf16[128,40,128]{2,0,1:T(8,128)(2,1)S(1)}, u32[]{:S(2)}, u32[]{:S(2)}) collective-permute-start(bf16[128,40,128]{2,0,1:T(8,128)(2,1)S(1)} %collective-permute-done.44), channel_id=1, source_target_pairs={{0,1},{1,2},{2,3},{3,4},{4,5},{5,6},{6,7},{7,8},{8,9},{9,10},{10,1... | collective-permute-start | bytes 3932168 | tf_op jit(solution)/shard_map/ppermute | solution.py:58
  412.3 28.1 %collective-permute-start.15 = (bf16[128,40,128]{2,0,1:T(8,128)(2,1)S(1)}, bf16[128,40,128]{2,0,1:T(8,128)(2,1)S(1)}, u32[]{:S(2)}, u32[]{:S(2)}) collective-permute-start(bf16[128,40,128]{2,0,1:T(8,128)(2,1)S(1)} %collective-permute-done.14), channel_id=1, source_target_pairs={{0,1},{1,2},{2,3},{3,4},{4,5},{5,6},{6,7},{7,8},{8,9},{9,10},{10,1... | collective-permute-start | bytes 3932168 | tf_op jit(solution)/shard_map/ppermute | solution.py:57
  426.3 28.1 %collective-permute-start.46 = (bf16[128,40,128]{2,0,1:T(8,128)(2,1)S(1)}, bf16[128,40,128]{2,0,1:T(8,128)(2,1)S(1)}, u32[]{:S(2)}, u32[]{:S(2)}) collective-permute-start(bf16[128,40,128]{2,0,1:T(8,128)(2,1)S(1)} %collective-permute-done.45), channel_id=1, source_target_pairs={{0,1},{1,2},{2,3},{3,4},{4,5},{5,6},{6,7},{7,8},{8,9},{9,10},{10,1... | collective-permute-start | bytes 3932168 | tf_op jit(solution)/shard_map/ppermute | solution.py:58
  440.4 28.1 %collective-permute-start.16 = (bf16[128,40,128]{2,0,1:T(8,128)(2,1)S(1)}, bf16[128,40,128]{2,0,1:T(8,128)(2,1)S(1)}, u32[]{:S(2)}, u32[]{:S(2)}) collective-permute-start(bf16[128,40,128]{2,0,1:T(8,128)(2,1)S(1)} %collective-permute-done.15), channel_id=1, source_target_pairs={{0,1},{1,2},{2,3},{3,4},{4,5},{5,6},{6,7},{7,8},{8,9},{9,10},{10,1... | collective-permute-start | bytes 3932168 | tf_op jit(solution)/shard_map/ppermute | solution.py:57
  454.4 28.1 %collective-permute-start.47 = (bf16[128,40,128]{2,0,1:T(8,128)(2,1)S(1)}, bf16[128,40,128]{2,0,1:T(8,128)(2,1)S(1)}, u32[]{:S(2)}, u32[]{:S(2)}) collective-permute-start(bf16[128,40,128]{2,0,1:T(8,128)(2,1)S(1)} %collective-permute-done.46), channel_id=1, source_target_pairs={{0,1},{1,2},{2,3},{3,4},{4,5},{5,6},{6,7},{7,8},{8,9},{9,10},{10,1... | collective-permute-start | bytes 3932168 | tf_op jit(solution)/shard_map/ppermute | solution.py:58
  468.5 28.1 %collective-permute-start.17 = (bf16[128,40,128]{2,0,1:T(8,128)(2,1)S(1)}, bf16[128,40,128]{2,0,1:T(8,128)(2,1)S(1)}, u32[]{:S(2)}, u32[]{:S(2)}) collective-permute-start(bf16[128,40,128]{2,0,1:T(8,128)(2,1)S(1)} %collective-permute-done.16), channel_id=1, source_target_pairs={{0,1},{1,2},{2,3},{3,4},{4,5},{5,6},{6,7},{7,8},{8,9},{9,10},{10,1... | collective-permute-start | bytes 3932168 | tf_op jit(solution)/shard_map/ppermute | solution.py:57
  510.6 28.1 %collective-permute-start.49 = (bf16[128,40,128]{2,0,1:T(8,128)(2,1)S(1)}, bf16[128,40,128]{2,0,1:T(8,128)(2,1)S(1)}, u32[]{:S(2)}, u32[]{:S(2)}) collective-permute-start(bf16[128,40,128]{2,0,1:T(8,128)(2,1)S(1)} %collective-permute-done.48), channel_id=1, source_target_pairs={{0,1},{1,2},{2,3},{3,4},{4,5},{5,6},{6,7},{7,8},{8,9},{9,10},{10,1... | collective-permute-start | bytes 3932168 | tf_op jit(solution)/shard_map/ppermute | solution.py:58
  552.7 28.1 %collective-permute-start.20 = (bf16[128,40,128]{2,0,1:T(8,128)(2,1)}, bf16[128,40,128]{2,0,1:T(8,128)(2,1)}, u32[]{:S(2)}, u32[]{:S(2)}) collective-permute-start(bf16[128,40,128]{2,0,1:T(8,128)(2,1)} %collective-permute-done.19), channel_id=1, source_target_pairs={{0,1},{1,2},{2,3},{3,4},{4,5},{5,6},{6,7},{7,8},{8,9},{9,10},{10,1... | collective-permute-start | bytes 3932168 | tf_op jit(solution)/shard_map/ppermute | solution.py:57
  566.8 28.1 %collective-permute-start.51 = (bf16[128,40,128]{2,0,1:T(8,128)(2,1)}, bf16[128,40,128]{2,0,1:T(8,128)(2,1)}, u32[]{:S(2)}, u32[]{:S(2)}) collective-permute-start(bf16[128,40,128]{2,0,1:T(8,128)(2,1)} %collective-permute-done.50), channel_id=1, source_target_pairs={{0,1},{1,2},{2,3},{3,4},{4,5},{5,6},{6,7},{7,8},{8,9},{9,10},{10,1... | collective-permute-start | bytes 3932168 | tf_op jit(solution)/shard_map/ppermute | solution.py:58
  580.8 28.1 %collective-permute-start.21 = (bf16[128,40,128]{2,0,1:T(8,128)(2,1)}, bf16[128,40,128]{2,0,1:T(8,128)(2,1)S(1)}, u32[]{:S(2)}, u32[]{:S(2)}) collective-permute-start(bf16[128,40,128]{2,0,1:T(8,128)(2,1)} %collective-permute-done.20), channel_id=1, source_target_pairs={{0,1},{1,2},{2,3},{3,4},{4,5},{5,6},{6,7},{7,8},{8,9},{9,10},{10,1... | collective-permute-start | bytes 3932168 | tf_op jit(solution)/shard_map/ppermute | solution.py:57
  594.9 28.1 %collective-permute-start.52 = (bf16[128,40,128]{2,0,1:T(8,128)(2,1)}, bf16[128,40,128]{2,0,1:T(8,128)(2,1)S(1)}, u32[]{:S(2)}, u32[]{:S(2)}) collective-permute-start(bf16[128,40,128]{2,0,1:T(8,128)(2,1)} %collective-permute-done.51), channel_id=1, source_target_pairs={{0,1},{1,2},{2,3},{3,4},{4,5},{5,6},{6,7},{7,8},{8,9},{9,10},{10,1... | collective-permute-start | bytes 3932168 | tf_op jit(solution)/shard_map/ppermute | solution.py:58
  608.9 28.1 %collective-permute-start.22 = (bf16[128,40,128]{2,0,1:T(8,128)(2,1)S(1)}, bf16[128,40,128]{2,0,1:T(8,128)(2,1)S(1)}, u32[]{:S(2)}, u32[]{:S(2)}) collective-permute-start(bf16[128,40,128]{2,0,1:T(8,128)(2,1)S(1)} %collective-permute-done.21), channel_id=1, source_target_pairs={{0,1},{1,2},{2,3},{3,4},{4,5},{5,6},{6,7},{7,8},{8,9},{9,10},{10,1... | collective-permute-start | bytes 3932168 | tf_op jit(solution)/shard_map/ppermute | solution.py:57
  637.0 28.1 %collective-permute-start.23 = (bf16[128,40,128]{2,0,1:T(8,128)(2,1)S(1)}, bf16[128,40,128]{2,0,1:T(8,128)(2,1)S(1)}, u32[]{:S(2)}, u32[]{:S(2)}) collective-permute-start(bf16[128,40,128]{2,0,1:T(8,128)(2,1)S(1)} %collective-permute-done.22), channel_id=1, source_target_pairs={{0,1},{1,2},{2,3},{3,4},{4,5},{5,6},{6,7},{7,8},{8,9},{9,10},{10,1... | collective-permute-start | bytes 3932168 | tf_op jit(solution)/shard_map/ppermute | solution.py:57
  665.1 28.1 %collective-permute-start.24 = (bf16[128,40,128]{2,0,1:T(8,128)(2,1)S(1)}, bf16[128,40,128]{2,0,1:T(8,128)(2,1)S(1)}, u32[]{:S(2)}, u32[]{:S(2)}) collective-permute-start(bf16[128,40,128]{2,0,1:T(8,128)(2,1)S(1)} %collective-permute-done.23), channel_id=1, source_target_pairs={{0,1},{1,2},{2,3},{3,4},{4,5},{5,6},{6,7},{7,8},{8,9},{9,10},{10,1... | collective-permute-start | bytes 3932168 | tf_op jit(solution)/shard_map/ppermute | solution.py:57
  693.2 28.1 %collective-permute-start.25 = (bf16[128,40,128]{2,0,1:T(8,128)(2,1)S(1)}, bf16[128,40,128]{2,0,1:T(8,128)(2,1)S(1)}, u32[]{:S(2)}, u32[]{:S(2)}) collective-permute-start(bf16[128,40,128]{2,0,1:T(8,128)(2,1)S(1)} %collective-permute-done.24), channel_id=1, source_target_pairs={{0,1},{1,2},{2,3},{3,4},{4,5},{5,6},{6,7},{7,8},{8,9},{9,10},{10,1... | collective-permute-start | bytes 3932168 | tf_op jit(solution)/shard_map/ppermute | solution.py:57
  721.3 28.1 %collective-permute-start.26 = (bf16[128,40,128]{2,0,1:T(8,128)(2,1)S(1)}, bf16[128,40,128]{2,0,1:T(8,128)(2,1)S(1)}, u32[]{:S(2)}, u32[]{:S(2)}) collective-permute-start(bf16[128,40,128]{2,0,1:T(8,128)(2,1)S(1)} %collective-permute-done.25), channel_id=1, source_target_pairs={{0,1},{1,2},{2,3},{3,4},{4,5},{5,6},{6,7},{7,8},{8,9},{9,10},{10,1... | collective-permute-start | bytes 3932168 | tf_op jit(solution)/shard_map/ppermute | solution.py:57
  777.5 28.1 %collective-permute-start.28 = (bf16[128,40,128]{2,0,1:T(8,128)(2,1)S(1)}, bf16[128,40,128]{2,0,1:T(8,128)(2,1)}, u32[]{:S(2)}, u32[]{:S(2)}) collective-permute-start(bf16[128,40,128]{2,0,1:T(8,128)(2,1)S(1)} %collective-permute-done.27), channel_id=1, source_target_pairs={{0,1},{1,2},{2,3},{3,4},{4,5},{5,6},{6,7},{7,8},{8,9},{9,10},{10,1... | collective-permute-start | bytes 3932168 | tf_op jit(solution)/shard_map/ppermute | solution.py:57
  805.5 28.1 %collective-permute-start.29 = (bf16[128,40,128]{2,0,1:T(8,128)(2,1)}, bf16[128,40,128]{2,0,1:T(8,128)(2,1)}, u32[]{:S(2)}, u32[]{:S(2)}) collective-permute-start(bf16[128,40,128]{2,0,1:T(8,128)(2,1)} %collective-permute-done.28), channel_id=1, source_target_pairs={{0,1},{1,2},{2,3},{3,4},{4,5},{5,6},{6,7},{7,8},{8,9},{9,10},{10,1... | collective-permute-start | bytes 3932168 | tf_op jit(solution)/shard_map/ppermute | solution.py:57
  833.6 28.1 %collective-permute-start.30 = (bf16[128,40,128]{2,0,1:T(8,128)(2,1)}, bf16[128,40,128]{2,0,1:T(8,128)(2,1)}, u32[]{:S(2)}, u32[]{:S(2)}) collective-permute-start(bf16[128,40,128]{2,0,1:T(8,128)(2,1)} %collective-permute-done.29), channel_id=1, source_target_pairs={{0,1},{1,2},{2,3},{3,4},{4,5},{5,6},{6,7},{7,8},{8,9},{9,10},{10,1... | collective-permute-start | bytes 3932168 | tf_op jit(solution)/shard_map/ppermute | solution.py:57
  847.7 211.5 %collective-permute-start.61 = (bf16[128,40,128]{2,0,1:T(8,128)(2,1)}, bf16[128,40,128]{2,0,1:T(8,128)(2,1)}, u32[]{:S(2)}, u32[]{:S(2)}) collective-permute-start(bf16[128,40,128]{2,0,1:T(8,128)(2,1)} %collective-permute-done.60), channel_id=1, source_target_pairs={{0,1},{1,2},{2,3},{3,4},{4,5},{5,6},{6,7},{7,8},{8,9},{9,10},{10,1... | collective-permute-start | bytes 3932168 | tf_op jit(solution)/shard_map/ppermute | solution.py:58
  (340 other events, 13285.6 us)
where the time goes:
time: 1090 us; the launch traced here: 1070 us
  waiting for transfers between devices  609 us (56%)
  matrix products  216 us (20%)
  starting transfers between devices  154 us (14%)
  other arithmetic  59.2 us (5%)
  local copies, waits for them, and re-layouts  27.8 us (3%)
    ppermute x31, waiting for transfers between devices, local(): kb = lax.ppermute(kb, axes, perm)  323 us
    ppermute x31, waiting for transfers between devices, local(): vb = lax.ppermute(vb, axes, perm)  286 us
    dot_general x65, matrix products, update(): jnp.einsum('grqk,kgd->grqd', p.astype(jnp.bfloat16), vc, preferred_elemen...  118 us
    dot_general x65, matrix products, update(): jnp.einsum('qgrd,kgd->grqk', qc, kc, preferred_element_type=jnp.float32)  97.6 us
    ppermute x31, starting transfers between devices, local(): kb = lax.ppermute(kb, axes, perm)  78.2 us
    ppermute x31, starting transfers between devices, local(): vb = lax.ppermute(vb, axes, perm)  75.6 us
    reduce_sum x33, other arithmetic, update(): l = alpha * l + jnp.sum(p, axis=-1)  36.5 us
    unnamed x654, local copies, waits for them, and re-layouts  25.8 us
  transfers between devices with their start and end apart: 62, of which 61 were waited for; matrix products, arithmetic and copies ran while one was open for 25% of the time, Pallas kernels for 0%

commit v1 on v0

v1 whole, which is shorter than its diff:
```python
import functools
import math

import jax
import jax.numpy as jnp
from jax import lax
from jax.experimental import pallas as pl
from jax.experimental.pallas import tpu as pltpu
from jax.sharding import PartitionSpec as P

MESH = pl.DeviceIdType.MESH
NEG = -1.0e30
TILE = 8
F32 = jnp.float32
BF16 = jnp.bfloat16


def kernel(ny, nx, nt, scale, q_hbm, k_hbm, v_hbm, o_hbm, tin, xs, send, qkv, sbuf, bias, ostage, orecv, ys, tout,
           in_sem, send_sem, recv_sem, fsend, frecv, osend, orecv_sem, out_sem):
    rows = q_hbm.shape[0]
    c2 = rows // 2
    hd = q_hbm.shape[2]
    ns = ny * nx
    cy = lax.axis_index("cy")
    cx = lax.axis_index("cx")
    x = cx // 2
    c = lax.rem(cx, 2)
    par = lax.rem(x + cy, 2)
    me = cy * nx + x
    pair = cy * (nx // 2) + x // 2
    nslots = (nt - par + 1) // 2

    def dev(s, core):
        return {"cy": s // nx, "cx": lax.rem(s, nx) * 2 + core}

    def in_copy(t, j):
        src = (q_hbm, k_hbm, v_hbm)[j]
        return pltpu.make_async_copy(src.at[:, pl.ds(pl.multiple_of(t * TILE, TILE), TILE), :], tin.at[t, j], in_sem.at[t, j])

    for t in range(nt):
        for j in range(3):
            in_copy(t, j).start()

    bar = pltpu.get_barrier_semaphore()

    def greet(i, _):
        pl.semaphore_signal(bar, inc=1, device_id=dev(lax.rem(me + i, ns), c), device_id_type=MESH)
        return 0

    lax.fori_loop(1, ns, greet, 0)
    pl.semaphore_signal(bar, inc=1, device_id=dev(me, 1 - c), device_id_type=MESH)

    qi = lax.broadcasted_iota(jnp.int32, (nx * c2, 2 * nx * c2), 0)
    ki = lax.broadcasted_iota(jnp.int32, (nx * c2, 2 * nx * c2), 1)
    qsp = 2 * (qi // c2) + c
    ksp = 2 * ((ki // c2) % nx) + ki // (nx * c2)
    qr = qi % c2
    kr = ki % c2
    low = (ksp < qsp) | ((ksp == qsp) & (kr <= qr))
    high = (ksp > qsp) | ((ksp == qsp) & (kr <= qr))
    bias[0] = jnp.where(low, 0.0, NEG)
    bias[1] = jnp.where(high, 0.0, NEG)

    def send_copy(t, k):
        yd = k // (nx // 2)
        xd = 2 * lax.rem(k, nx // 2) + lax.rem(yd + t, 2)
        d = yd * nx + xd
        slot = t // 2
        return d, slot, pltpu.make_async_remote_copy(
            src_ref=send.at[t, k], dst_ref=qkv.at[slot, c, me], send_sem=send_sem.at[t, k],
            recv_sem=recv_sem.at[slot, me], device_id=dev(d, c), device_id_type=MESH)

    def send_tile(t, _):
        for j in range(3):
            in_copy(t, j).wait()
            xs[j] = tin[t, j].astype(F32).reshape(rows * TILE, hd)

        def one(i, _):
            yd = lax.rem(cy + i // (nx // 2), ny)
            k = yd * (nx // 2) + lax.rem(x // 2 + i, nx // 2)
            d, slot, cp = send_copy(t, k)
            for j in range(3):
                send[t, k, j] = xs[j, pl.ds(k, rows, stride=TILE), :].astype(BF16).reshape(2, c2, hd)

            @pl.when(d != me)
            def _():
                cp.start()

            @pl.when(d == me)
            def _():
                qkv[slot, c, me] = send[t, k]
            return 0

        lax.fori_loop(0, TILE, one, 0)
        return 0

    pl.semaphore_wait(bar, ns)
    lax.fori_loop(0, nt, send_tile, 0)

    def fwd_copy(slot, s, core):
        return pltpu.make_async_remote_copy(
            src_ref=qkv.at[slot, core, s, pl.ds(1, 2)], dst_ref=qkv.at[slot, core, s, pl.ds(1, 2)],
            send_sem=fsend.at[slot, s], recv_sem=frecv.at[slot, s], device_id=dev(me, 1 - c), device_id_type=MESH)

    def recv_copy(slot, s):
        return pltpu.make_async_remote_copy(
            src_ref=qkv.at[slot, c, s], dst_ref=qkv.at[slot, c, s], send_sem=send_sem.at[0, 0],
            recv_sem=recv_sem.at[slot, s], device_id=dev(me, 1 - c), device_id_type=MESH)

    def o_copy(slot, s):
        t = 2 * slot + par
        return pltpu.make_async_remote_copy(
            src_ref=ostage.at[slot, s], dst_ref=orecv.at[t, pair], send_sem=osend.at[slot, s],
            recv_sem=orecv_sem.at[t, pair], device_id=dev(s, c), device_id_type=MESH)

    def band(slot, b, j):
        half = b // ny
        yk = jnp.where(half == 0, b, 2 * ny - 1 - b)
        return qkv[slot, :, pl.ds(nx * yk, nx), j, half].reshape(2 * nx * c2, hd)

    def scores(q, k):
        return lax.dot_general(q, k, (((1,), (1,)), ((), ())), preferred_element_type=F32) * scale

    def lanes(s, op):
        r = s[:, :hd]
        for i in range(1, s.shape[1] // hd):
            r = op(r, s[:, i * hd:(i + 1) * hd])
        return r

    def attend(slot, y, half):
        j = y if half == 0 else 2 * ny - 1 - y
        q = qkv[slot, c, pl.ds(nx * y, nx), 0, half].reshape(nx * c2, hd)
        s = scores(q, band(slot, j, 1)) + bias[half]
        sbuf[j] = s
        mx = lanes(s, jnp.maximum)

        def first(b, mx):
            s = scores(q, band(slot, b, 1))
            sbuf[b] = s
            return jnp.maximum(mx, lanes(s, jnp.maximum))

        mx = lax.fori_loop(0, j, first, mx)
        m = jnp.max(mx, axis=-1, keepdims=True)

        def second(b, carry):
            l, acc = carry
            p = jnp.exp2(sbuf[b] - m)
            l = l + lanes(p, jnp.add)
            acc = acc + jnp.dot(p.astype(BF16), band(slot, b, 2), preferred_element_type=F32)
            return l, acc

        zero = jnp.zeros((nx * c2, hd), F32)
        l, acc = lax.fori_loop(0, j + 1, second, (zero, zero))
        o = acc / jnp.sum(l, axis=-1, keepdims=True)
        ostage[slot, pl.ds(nx * y, nx), half] = o.astype(BF16).reshape(nx, c2, hd)

    def do_slot(slot, _):
        def forward(s, _):
            @pl.when(s != me)
            def _():
                recv_copy(slot, s).wait_recv()

            fwd_copy(slot, s, c).start()
            return 0

        lax.fori_loop(0, ns, forward, 0)

        def arrived(s, _):
            fwd_copy(slot, s, 1 - c).wait_recv()
            return 0

        lax.fori_loop(0, ns, arrived, 0)

        def rows_of(y, _):
            attend(slot, y, 0)
            attend(slot, y, 1)

            def back(i, _):
                s = nx * y + i

                @pl.when(s != me)
                def _():
                    o_copy(slot, s).start()

                @pl.when(s == me)
                def _():
                    orecv[2 * slot + par, pair] = ostage[slot, s]
                return 0

            lax.fori_loop(0, nx, back, 0)
            return 0

        lax.fori_loop(0, ny, rows_of, 0)
        return 0

    lax.fori_loop(0, nslots, do_slot, 0)

    def out_copy(t):
        return pltpu.make_async_copy(tout.at[t], o_hbm.at[:, pl.ds(pl.multiple_of(t * TILE, TILE), TILE), :], out_sem.at[t])

    def out_tile(t, _):
        def one(k, _):
            yd = k // (nx // 2)
            d = yd * nx + 2 * lax.rem(k, nx // 2) + lax.rem(yd + t, 2)

            @pl.when(d != me)
            def _():
                pltpu.make_async_remote_copy(
                    src_ref=orecv.at[t, k], dst_ref=orecv.at[t, k], send_sem=osend.at[0, 0],
                    recv_sem=orecv_sem.at[t, k], device_id=dev(me, 1 - c), device_id_type=MESH).wait_recv()

            ys[pl.ds(k, rows, stride=TILE), :] = orecv[t, k].reshape(rows, hd).astype(F32)
            return 0

        lax.fori_loop(0, TILE, one, 0)
        tout[t] = ys[...].reshape(rows, TILE, hd).astype(BF16)
        out_copy(t).start()
        return 0

    lax.fori_loop(0, nt, out_tile, 0)

    def sent(t, _):
        def one(k, _):
            d, slot, cp = send_copy(t, k)

            @pl.when(d != me)
            def _():
                cp.wait_send()
            return 0

        lax.fori_loop(0, TILE, one, 0)
        out_copy(t).wait()
        return 0

    lax.fori_loop(0, nt, sent, 0)

    def drained(slot, _):
        def one(s, _):
            fwd_copy(slot, s, c).wait_send()

            @pl.when(s != me)
            def _():
                o_copy(slot, s).wait_send()
            return 0

        lax.fori_loop(0, ns, one, 0)
        return 0

    lax.fori_loop(0, nslots, drained, 0)


def solution(mesh):
    ny = mesh.shape['cy']
    nx = mesh.shape['cx'] // 2
    spec = P(('dp', 'cy', 'cx'))

    def local(q, k, v):
        rows, nh, hd = q.shape
        c2 = rows // 2
        nt = nh // TILE
        ns = ny * nx
        nslot = (nt + 1) // 2
        scale = hd ** -0.5 * math.log2(math.e)
        dma = pltpu.SemaphoreType.DMA
        return pl.pallas_call(
            functools.partial(kernel, ny, nx, nt, scale),
            out_shape=jax.ShapeDtypeStruct(q.shape, q.dtype),
            in_specs=[pl.BlockSpec(memory_space=pl.ANY)] * 3,
            out_specs=pl.BlockSpec(memory_space=pl.ANY),
            scratch_shapes=[
                pltpu.VMEM((nt, 3, rows, TILE, hd), BF16),
                pltpu.VMEM((3, rows * TILE, hd), F32),
                pltpu.VMEM((nt, TILE, 3, 2, c2, hd), BF16),
                pltpu.VMEM((nslot, 2, ns, 3, 2, c2, hd), BF16),
                pltpu.VMEM((2 * ny, nx * c2, 2 * nx * c2), F32),
                pltpu.VMEM((2, nx * c2, 2 * nx * c2), F32),
                pltpu.VMEM((nslot, ns, 2, c2, hd), BF16),
                pltpu.VMEM((nt, TILE, 2, c2, hd), BF16),
                pltpu.VMEM((rows * TILE, hd), F32),
                pltpu.VMEM((nt, rows, TILE, hd), BF16),
                dma((nt, 3)), dma((nt, TILE)), dma((nslot, ns)), dma((nslot, ns)), dma((nslot, ns)),
                dma((nslot, ns)), dma((nt, TILE)), dma((nt,)),
            ],
            compiler_params=pltpu.CompilerParams(collective_id=0, has_side_effects=True, vmem_limit_bytes=56 * 1024 * 1024),
        )(q, k, v)

    return jax.shard_map(local, mesh=mesh, in_specs=(spec, spec, spec), out_specs=spec, check_vma=False)
```

time: 1090 us -> 103 us (0.09); the launches traced: 1070 us -> 103 us
  waiting for transfers between devices: 609 us -> 0 us
  matrix products: 216 us -> 0 us
  starting transfers between devices: 154 us -> 0 us
  Pallas kernels: 0 us -> 100 us
  other arithmetic: 59.2 us -> 0 us
  local copies, waits for them, and re-layouts: 27.8 us -> 2.49 us
    ppermute x62 -> x0, waiting for transfers between devices: 609 us -> none  [the longest x31 323 us: local(): kb = lax.ppermute(kb, axes, perm)]
    dot_general x130 -> x0, matrix products: 216 us -> none  [the longest x65 118 us: update(): jnp.einsum('grqk,kgd->grqd', p.astype(jnp.bfloat16), vc, preferred_elemen...]
    ppermute x62 -> x0, starting transfers between devices: 154 us -> none  [the longest x31 78.2 us: local(): kb = lax.ppermute(kb, axes, perm)]
    pallas_call x0 -> x1, Pallas kernels: none -> 100 us  [local(): pl.pallas_call(functools.partial(kernel, ny, nx, nt, scale), out_shape=ja...]
    reduce_sum x33 -> x0, other arithmetic: 36.5 us -> none  [update(): l = alpha * l + jnp.sum(p, axis=-1)]
    unnamed x654 -> x1, local copies, waits for them, and re-layouts: 25.8 us -> 2.49 us
    add x15 -> x0, other arithmetic: 15.2 us -> none  [update(): l = alpha * l + jnp.sum(p, axis=-1)]
  transfers between devices with their start and end apart: 62 -> 0, of which waited for: 61 -> 0; matrix products, arithmetic and copies ran while one was open for 25% -> 0% of each run, Pallas kernels for 0% -> 0%
where the time goes in v1:
time: 103 us
  Pallas kernels  100 us (97%)
  local copies, waits for them, and re-layouts  2.49 us (2%)
    pallas_call x1, Pallas kernels, local(): pl.pallas_call(functools.partial(kernel, ny, nx, nt, scale), out_shape=ja...  100 us
    unnamed x1, local copies, waits for them, and re-layouts  2.49 us

profile of v1, /device:TPU:97, one launch (start us, length us, event | category | flops | bytes accessed | tf_op | source)
XLA Modules:
  0.0 102.7 jit_solution(5807941912263986294)
XLA Ops:
  0.0 100.2 %shard_map.37 = bf16[128,40,128]{2,1,0:T(8,128)(2,1)} custom-call(bf16[128,40,128]{2,1,0:T(8,128)(2,1)} %q_hbm.1, bf16[128,40,128]{2,1,0:T(8,128)(2,1)} %k_hbm.1, bf16[128,40,128]{2,1,0:T(8,128)(2,1)} %v_hbm.1), custom_call_target="tpu_custom_call" | custom-call | tf_op jit(solution)/shard_map/pallas_call | solution.py:265
  100.2 2.5 %copy.5 = bf16[128,40,128]{2,1,0:T(8,128)(2,1)} copy(bf16[128,40,128]{2,1,0:T(8,128)(2,1)} %shard_map.37) | data formatting | bytes 2621440

commit v2 on v1

--- a/solution.py
+++ b/solution.py
@@ -15,7 +15,7 @@
 BF16 = jnp.bfloat16
 
 
-def kernel(ny, nx, nt, scale, q_hbm, k_hbm, v_hbm, o_hbm, tin, xs, send, qkv, sbuf, bias, ostage, orecv, ys, tout,
+def kernel(ny, nx, nt, scale, q_hbm, k_hbm, v_hbm, o_hbm, tin, xs, send, qkv, sbuf, bias, mbuf, lbuf, abuf, ostage, orecv, ys, tout,
            in_sem, send_sem, recv_sem, fsend, frecv, osend, orecv_sem, out_sem):
     rows = q_hbm.shape[0]
     c2 = rows // 2
@@ -127,32 +127,35 @@
             r = op(r, s[:, i * hd:(i + 1) * hd])
         return r
 
-    def attend(slot, y, half):
-        j = y if half == 0 else 2 * ny - 1 - y
-        q = qkv[slot, c, pl.ds(nx * y, nx), 0, half].reshape(nx * c2, hd)
-        s = scores(q, band(slot, j, 1)) + bias[half]
-        sbuf[j] = s
-        mx = lanes(s, jnp.maximum)
-
-        def first(b, mx):
+    def attend(slot, y):
+        last = 2 * ny - 1
+        blocks = [(0, y, 0), (1, last - y, 1)]
+        for n in range(last):
+            high = (n >= y).astype(jnp.int32)
+            blocks.append((high, n - high * y, None))
+        for n, (half, b, mask) in enumerate(blocks):
+            q = qkv[slot, c, pl.ds(nx * y, nx), 0, half].reshape(nx * c2, hd)
             s = scores(q, band(slot, b, 1))
-            sbuf[b] = s
-            return jnp.maximum(mx, lanes(s, jnp.maximum))
-
-        mx = lax.fori_loop(0, j, first, mx)
-        m = jnp.max(mx, axis=-1, keepdims=True)
-
-        def second(b, carry):
-            l, acc = carry
-            p = jnp.exp2(sbuf[b] - m)
-            l = l + lanes(p, jnp.add)
-            acc = acc + jnp.dot(p.astype(BF16), band(slot, b, 2), preferred_element_type=F32)
-            return l, acc
-
-        zero = jnp.zeros((nx * c2, hd), F32)
-        l, acc = lax.fori_loop(0, j + 1, second, (zero, zero))
-        o = acc / jnp.sum(l, axis=-1, keepdims=True)
-        ostage[slot, pl.ds(nx * y, nx), half] = o.astype(BF16).reshape(nx, c2, hd)
+            if mask is not None:
+                s = s + bias[mask]
+            sbuf[n] = s
+            mx = lanes(s, jnp.maximum)
+            mbuf[half] = mx if mask is not None else jnp.maximum(mbuf[half], mx)
+        for half in range(2):
+            mbuf[half] = jnp.broadcast_to(jnp.max(mbuf[half], axis=-1, keepdims=True), (nx * c2, hd))
+        for n, (half, b, mask) in enumerate(blocks):
+            m = mbuf[half]
+            p = jnp.exp2(sbuf[n] - jnp.concatenate([m] * (sbuf.shape[2] // hd), axis=1))
+            l = lanes(p, jnp.add)
+            pv = jnp.dot(p.astype(BF16), band(slot, b, 2), preferred_element_type=F32)
+            if mask is None:
+                l = lbuf[half] + l
+                pv = abuf[half] + pv
+            lbuf[half] = l
+            abuf[half] = pv
+        for half in range(2):
+            o = abuf[half] / jnp.sum(lbuf[half], axis=-1, keepdims=True)
+            ostage[slot, pl.ds(nx * y, nx), half] = o.astype(BF16).reshape(nx, c2, hd)
 
     def do_slot(slot, _):
         def forward(s, _):
@@ -172,8 +175,7 @@
         lax.fori_loop(0, ns, arrived, 0)
 
         def rows_of(y, _):
-            attend(slot, y, 0)
-            attend(slot, y, 1)
+            attend(slot, y)
 
             def back(i, _):
                 s = nx * y + i
@@ -272,8 +274,11 @@
                 pltpu.VMEM((3, rows * TILE, hd), F32),
                 pltpu.VMEM((nt, TILE, 3, 2, c2, hd), BF16),
                 pltpu.VMEM((nslot, 2, ns, 3, 2, c2, hd), BF16),
-                pltpu.VMEM((2 * ny, nx * c2, 2 * nx * c2), F32),
+                pltpu.VMEM((2 * ny + 1, nx * c2, 2 * nx * c2), F32),
                 pltpu.VMEM((2, nx * c2, 2 * nx * c2), F32),
+                pltpu.VMEM((2, nx * c2, hd), F32),
+                pltpu.VMEM((2, nx * c2, hd), F32),
+                pltpu.VMEM((2, nx * c2, hd), F32),
                 pltpu.VMEM((nslot, ns, 2, c2, hd), BF16),
                 pltpu.VMEM((nt, TILE, 2, c2, hd), BF16),
                 pltpu.VMEM((rows * TILE, hd), F32),

time: 103 us -> 90.7 us (0.88)
  Pallas kernels: 100 us -> 88.1 us
    pallas_call x1, Pallas kernels: 100 us -> 88.1 us  [local(): pl.pallas_call(functools.partial(kernel, ny, nx, nt, scale), out_shape=ja...]
where the time goes in v2:
time: 90.7 us; the launch traced here: 90.6 us
  Pallas kernels  88.1 us (97%)
  local copies, waits for them, and re-layouts  2.49 us (3%)
    pallas_call x1, Pallas kernels, local(): pl.pallas_call(functools.partial(kernel, ny, nx, nt, scale), out_shape=ja...  88.1 us
    unnamed x1, local copies, waits for them, and re-layouts  2.49 us

profile of v2, /device:TPU:97, one launch (start us, length us, event | category | flops | bytes accessed | tf_op | source)
XLA Modules:
  0.0 90.6 jit_solution(4549225459184032107)
XLA Ops:
  0.0 88.1 %shard_map.37 = bf16[128,40,128]{2,1,0:T(8,128)(2,1)} custom-call(bf16[128,40,128]{2,1,0:T(8,128)(2,1)} %q_hbm.1, bf16[128,40,128]{2,1,0:T(8,128)(2,1)} %k_hbm.1, bf16[128,40,128]{2,1,0:T(8,128)(2,1)} %v_hbm.1), custom_call_target="tpu_custom_call" | custom-call | tf_op jit(solution)/shard_map/pallas_call | solution.py:267
  88.1 2.5 %copy.5 = bf16[128,40,128]{2,1,0:T(8,128)(2,1)} copy(bf16[128,40,128]{2,1,0:T(8,128)(2,1)} %shard_map.37) | data formatting | bytes 2621440

commit v3 on v1

v3 whole, which is shorter than its diff:
```python
import functools
import math

import jax
import jax.numpy as jnp
from jax import lax
from jax.experimental import pallas as pl
from jax.experimental.pallas import tpu as pltpu
from jax.sharding import PartitionSpec as P

MESH = pl.DeviceIdType.MESH
NEG = -1.0e30
TILE = 8
F32 = jnp.float32
BF16 = jnp.bfloat16


def kernel(ny, nx, nt, scale, q_hbm, k_hbm, v_hbm, o_hbm, tin, xs, send, r1, qkv, sbuf, bias, ostage, orecv, ys, tout,
           in_sem, s1, q1, s2, q2, sx, fsend, frecv, osend, orecv_sem, out_sem):
    rows = q_hbm.shape[0]
    c2 = rows // 2
    hd = q_hbm.shape[2]
    cy = lax.axis_index("cy")
    cx = lax.axis_index("cx")
    x = cx // 2
    c = lax.rem(cx, 2)
    odd = lax.rem(x + cy, 2)
    mate = cy + 1 - 2 * lax.rem(cy, 2)
    across = ny - 1 - cy
    inner = lax.rem((cy + 1) // 2, 2)

    def dev(xd, yd, core):
        return {"cy": yd, "cx": xd * 2 + core}

    nslot = (nt - 1) // 2

    def slot_of(t):
        return jnp.where(t == 0, nslot, (t - 1) // 2)

    def owner_row(t, xd, h, y, inn):
        shared = jnp.where(inn == h, y, y + 1 - 2 * lax.rem(y, 2))
        return jnp.where(t == 0, shared, lax.rem(xd + t, 2) + 2 * h)

    def in_copy(t, j):
        src = (q_hbm, k_hbm, v_hbm)[j]
        return pltpu.make_async_copy(src.at[:, pl.ds(pl.multiple_of(t * TILE, TILE), TILE), :], tin.at[t, j], in_sem.at[t, j])

    bar = pltpu.get_barrier_semaphore()
    for i in range(1, nx):
        pl.semaphore_signal(bar, inc=1, device_id=dev(lax.rem(x + i, nx), cy, c), device_id_type=MESH)
    for i in range(1, ny):
        pl.semaphore_signal(bar, inc=1, device_id=dev(x, lax.rem(cy + i, ny), c), device_id_type=MESH)
    pl.semaphore_signal(bar, inc=1, device_id=dev(x, cy, 1 - c), device_id_type=MESH)

    for t in range(nt):
        for j in range(3):
            in_copy(t, j).start()

    def x_copy(t, xd):
        return pltpu.make_async_remote_copy(
            src_ref=send.at[t, xd], dst_ref=r1.at[t, x], send_sem=s1.at[t, xd], recv_sem=q1.at[t, x],
            device_id=dev(xd, cy, c), device_id_type=MESH)

    def gray(i):
        return jnp.where(i < 2, i, 5 - i)

    def load_tile(t, u):
        for j in range(3):
            in_copy(t, j).wait()
            xs[u, j] = tin[t, j].astype(F32).reshape(rows * TILE, hd)

    def head_rows(u, j, k):
        return xs[u, j, pl.ds(k, rows, stride=TILE), :].astype(BF16).reshape(2, c2, hd)

    def send_tiles(t, n):
        def one(i, _):
            xd = lax.rem(x + gray(i), nx)
            for u in range(n):
                for h in range(2):
                    for j in range(3):
                        send[t + u, xd, h, j] = head_rows(u, j, 2 * xd + h)
                x_copy(t + u, xd).start()
            return 0

        lax.fori_loop(1, nx, one, 0)
        for u in range(n):
            for h in range(2):
                for j in range(3):
                    r1[t + u, x, h, j] = head_rows(u, j, 2 * x + h)

    load_tile(0, 0)

    qi = lax.broadcasted_iota(jnp.int32, (nx * c2, 2 * nx * c2), 0)
    ki = lax.broadcasted_iota(jnp.int32, (nx * c2, 2 * nx * c2), 1)
    qsp = 2 * (qi // c2) + c
    ksp = 2 * ((ki // c2) % nx) + ki // (nx * c2)
    qr = qi % c2
    kr = ki % c2
    low = (ksp < qsp) | ((ksp == qsp) & (kr <= qr))
    high = (ksp > qsp) | ((ksp == qsp) & (kr <= qr))
    bias[0] = jnp.where(low, 0.0, NEG)
    bias[1] = jnp.where(high, 0.0, NEG)

    pl.semaphore_wait(bar, nx + ny - 1)
    send_tiles(0, 1)

    def send_rest(i, _):
        load_tile(2 * i + 1, 0)
        load_tile(2 * i + 2, 1)
        send_tiles(2 * i + 1, 2)
        return 0

    lax.fori_loop(0, nslot, send_rest, 0)

    def y_copy(t, sx_, h, yd):
        slot = slot_of(t)
        return pltpu.make_async_remote_copy(
            src_ref=r1.at[t, sx_, h], dst_ref=qkv.at[slot, c, cy, sx_], send_sem=s2.at[t, sx_, h],
            recv_sem=q2.at[slot, cy, sx_], device_id=dev(x, yd, c), device_id_type=MESH)

    def y_recv(slot, sy, sx_):
        return pltpu.make_async_remote_copy(
            src_ref=qkv.at[slot, c, sy, sx_], dst_ref=qkv.at[slot, c, sy, sx_], send_sem=s2.at[0, 0, 0],
            recv_sem=q2.at[slot, sy, sx_], device_id=dev(x, cy, 1 - c), device_id_type=MESH)

    def kv_view(ref, full):
        return ref.at[pl.ds(1, 2)] if full else ref.at[pl.ds(1, 2), 0]

    def cross_copy(src, sy, sx_, full):
        return pltpu.make_async_remote_copy(
            src_ref=kv_view(src, full), dst_ref=kv_view(qkv.at[nslot, c, sy, sx_], full), send_sem=sx.at[sy, sx_],
            recv_sem=q2.at[nslot, sy, sx_], device_id=dev(x, across, c), device_id_type=MESH)

    def core_copy(src, slot, sy, sx_, core, full):
        return pltpu.make_async_remote_copy(
            src_ref=kv_view(src, full), dst_ref=kv_view(qkv.at[slot, core, sy, sx_], full), send_sem=fsend.at[slot, sy, sx_],
            recv_sem=frecv.at[slot, sy, sx_], device_id=dev(x, cy, 1 - c), device_id_type=MESH)

    def either(full, act):
        @pl.when(full)
        def _():
            act(True)

        @pl.when(jnp.logical_not(full))
        def _():
            act(False)

    outer = cy < ny // 2

    def cross(src, sy, sx_):
        either(jnp.logical_not(outer), lambda full: cross_copy(src, sy, sx_, full).start())

    def relay(t, i):
        sx_ = lax.rem(x + gray(i), nx)

        @pl.when(sx_ != x)
        def _():
            pltpu.make_async_remote_copy(
                src_ref=send.at[t, 0], dst_ref=r1.at[t, sx_], send_sem=s1.at[0, 0], recv_sem=q1.at[t, sx_],
                device_id=dev(x, cy, 1 - c), device_id_type=MESH).wait_recv()

        slot = slot_of(t)
        for h in range(2):
            yd = owner_row(t, x, h, cy, inner)

            @pl.when(yd != cy)
            def _():
                y_copy(t, sx_, h, yd).start()

            @pl.when(yd == cy)
            def _():
                core_copy(r1.at[t, sx_, h], slot, cy, sx_, c, True).start()

                @pl.when(t == 0)
                def _():
                    cross(r1.at[t, sx_, h], cy, sx_)

                qkv[slot, c, cy, sx_] = r1[t, sx_, h]

    def share_first(i):
        sx_ = lax.rem(x + gray(i), nx)
        y_recv(nslot, mate, sx_).wait_recv()
        core_copy(qkv.at[nslot, c, mate, sx_], nslot, mate, sx_, c, True).start()
        cross(qkv.at[nslot, c, mate, sx_], mate, sx_)

    def share_second(i):
        sx_ = lax.rem(x + gray(i), nx)
        for sy in (across, across + 1 - 2 * lax.rem(across, 2)):
            def act(full):
                cross_copy(qkv.at[nslot, c, sy, sx_], sy, sx_, full).wait_recv()
                core_copy(qkv.at[nslot, c, sy, sx_], nslot, sy, sx_, c, full).start()

            either(outer, act)
        return 0

    def full_rows(slot, sy):
        return (slot < nslot) | outer | (sy >= ny // 2)

    def arrived(slot):
        def one(i, _):
            sy = i // nx
            sx_ = lax.rem(i, nx)
            either(full_rows(slot, sy), lambda full: core_copy(qkv.at[slot, 1 - c, sy, sx_], slot, sy, sx_, 1 - c, full).wait_recv())
            return 0

        lax.fori_loop(0, nx * ny, one, 0)

    def gather(slot):
        def one(i, _):
            sy = lax.rem(cy + i // nx, ny)
            sx_ = lax.rem(x + gray(lax.rem(i, nx)), nx)
            y_recv(slot, sy, sx_).wait_recv()
            core_copy(qkv.at[slot, c, sy, sx_], slot, sy, sx_, c, True).start()
            return 0

        lax.fori_loop(nx, nx * ny, one, 0)

    def tile_of(slot):
        return jnp.where(slot == nslot, 0, 2 * slot + 2 - odd)

    def my_head(slot):
        return 2 * x + jnp.where(slot == nslot, inner, cy // 2)

    def o_copy(slot, sy, sx_):
        t = tile_of(slot)
        k = my_head(slot)
        return pltpu.make_async_remote_copy(
            src_ref=ostage.at[slot, sy, sx_], dst_ref=orecv.at[t, k], send_sem=osend.at[slot, sy, sx_],
            recv_sem=orecv_sem.at[t, k], device_id=dev(sx_, sy, c), device_id_type=MESH)

    def band(slot, b, j):
        half = b // ny
        yk = b if half == 0 else 2 * ny - 1 - b
        return qkv[slot, :, yk, :, j, half].reshape(2 * nx * c2, hd)

    def scores(q, k):
        return lax.dot_general(q, k, (((1,), (1,)), ((), ())), preferred_element_type=F32) * scale

    def lanes(s, op):
        r = s[:, :hd]
        for i in range(1, s.shape[1] // hd):
            r = op(r, s[:, i * hd:(i + 1) * hd])
        return r

    def attend(slot, pair):
        for p in range(ny // 2):
            @pl.when(pair == p)
            def _():
                attend_rows(slot, (2 * p, 2 * p + 1))

    def attend_rows(slot, source_rows):
        tiles = [(y, half, 2 * ny - y if half else y + 1) for half in (1, 0) for y in source_rows]
        tiles.sort(key=lambda t: -t[2])
        start = [sum(t[2] for t in tiles[:i]) for i in range(len(tiles) + 1)]
        top = [None] * len(tiles)
        total = [None] * len(tiles)

        def score(i, b):
            y, half, nb = tiles[i]
            q = qkv[slot, c, y, :, 0, half].reshape(nx * c2, hd)
            s = scores(q, band(slot, b, 1))
            if b == nb - 1:
                s = s + bias[half]
            sbuf[start[i] + b] = s
            t = lanes(s, jnp.maximum)
            top[i] = t if top[i] is None else jnp.maximum(top[i], t)

        def weigh(i, b, m):
            p = jnp.exp2(sbuf[start[i] + b] - m)
            l = lanes(p, jnp.add)
            pv = jnp.dot(p.astype(BF16), band(slot, b, 2), preferred_element_type=F32)
            total[i] = (l, pv) if total[i] is None else (total[i][0] + l, total[i][1] + pv)

        for b in range(tiles[0][2]):
            score(0, b)
        for i, (y, half, nb) in enumerate(tiles):
            m = jnp.broadcast_to(jnp.max(top[i], axis=-1, keepdims=True), (nx * c2, hd))
            m = jnp.concatenate([m] * (sbuf.shape[2] // hd), axis=1)
            nxt = tiles[i + 1][2] if i + 1 < len(tiles) else 0
            for b in range(max(nb, nxt)):
                if b < nxt:
                    score(i + 1, b)
                if b < nb:
                    weigh(i, b, m)
            l, acc = total[i]
            o = acc / jnp.sum(l, axis=-1, keepdims=True)
            ostage[slot, y, :, half] = o.astype(BF16).reshape(nx, c2, hd)

    def send_back(slot, y):
        def back(sx_, _):
            mine = (sx_ == x) & (y == cy)

            @pl.when(jnp.logical_not(mine))
            def _():
                o_copy(slot, y, sx_).start()

            @pl.when(mine)
            def _():
                orecv[tile_of(slot), my_head(slot)] = ostage[slot, y, sx_]
            return 0

        lax.fori_loop(0, nx, back, 0)
        return 0

    def relay_two(n, i):
        relay(2 * n + 1, i)
        relay(2 * n + 2, i)

    relay(0, 0)
    relay_two(0, 0)

    def first(i, _):
        @pl.when(i < nx)
        def _():
            relay(0, i)

        @pl.when(i == nx - 1)
        def _():
            relay_two(1, 0)

        share_first(i - 1)
        return 0

    lax.fori_loop(1, nx + 1, first, 0)
    lax.fori_loop(1, nx, lambda i, _: (relay_two(0, i), 0)[1], 0)
    lax.fori_loop(0, nx, lambda i, _: share_second(i), 0)

    def step(n, _):
        pairs = ny // 2
        slot = jnp.where(n == 0, nslot, (n - 1) // pairs)
        pair = jnp.where(n == 0, cy // 2, lax.rem(n + 1, pairs))

        @pl.when(n == 0)
        def _():
            relay_two(1, 1)
            relay_two(1, 2)

        @pl.when(n == 1)
        def _():
            relay_two(1, 3)

        @pl.when((n == 1) | (n == 1 + pairs))
        def _():
            gather(slot)

        @pl.when(n != 2)
        def _():
            @pl.when(n != 2 + pairs)
            def _():
                arrived(slot)

        attend(slot, pair)
        send_back(slot, 2 * pair)
        send_back(slot, 2 * pair + 1)
        return 0

    lax.fori_loop(0, 1 + nslot * ny // 2, step, 0)

    def out_copy(t):
        return pltpu.make_async_copy(tout.at[t], o_hbm.at[:, pl.ds(pl.multiple_of(t * TILE, TILE), TILE), :], out_sem.at[t])

    def out_tile(t, _):
        def one(k, _):
            xd = k // 2
            yd = owner_row(t, xd, lax.rem(k, 2), cy, inner)

            @pl.when((xd != x) | (yd != cy))
            def _():
                pltpu.make_async_remote_copy(
                    src_ref=orecv.at[t, k], dst_ref=orecv.at[t, k], send_sem=osend.at[0, 0, 0],
                    recv_sem=orecv_sem.at[t, k], device_id=dev(x, cy, 1 - c), device_id_type=MESH).wait_recv()

            ys[pl.ds(k, rows, stride=TILE), :] = orecv[t, k].reshape(rows, hd).astype(F32)
            return 0

        lax.fori_loop(0, TILE, one, 0)
        tout[t] = ys[...].reshape(rows, TILE, hd).astype(BF16)
        out_copy(t).start()
        return 0

    lax.fori_loop(0, nt, out_tile, 0)

    def sent(t, _):
        def one(i, _):
            xd = lax.rem(x + i, nx)

            @pl.when(i > 0)
            def _():
                x_copy(t, xd).wait_send()

            for h in range(2):
                yd = owner_row(t, x, h, cy, inner)

                @pl.when(yd != cy)
                def _():
                    y_copy(t, xd, h, yd).wait_send()
            return 0

        lax.fori_loop(0, nx, one, 0)
        out_copy(t).wait()
        return 0

    lax.fori_loop(0, nt, sent, 0)

    def drained(slot, _):
        def one(i, _):
            sy = i // nx
            sx_ = lax.rem(i, nx)
            mine = (sy // 2) == (cy // 2)
            either(full_rows(slot, sy), lambda full: core_copy(qkv.at[slot, c, sy, sx_], slot, sy, sx_, c, full).wait_send())

            @pl.when((slot == nslot) & mine)
            def _():
                either(jnp.logical_not(outer), lambda full: cross_copy(qkv.at[nslot, c, sy, sx_], sy, sx_, full).wait_send())

            @pl.when(((slot < nslot) | mine) & ((sy != cy) | (sx_ != x)))
            def _():
                o_copy(slot, sy, sx_).wait_send()
            return 0

        lax.fori_loop(0, nx * ny, one, 0)
        return 0

    lax.fori_loop(0, nslot + 1, drained, 0)


def solution(mesh):
    ny = mesh.shape['cy']
    nx = mesh.shape['cx'] // 2
    spec = P(('dp', 'cy', 'cx'))

    def local(q, k, v):
        rows, nh, hd = q.shape
        c2 = rows // 2
        nt = nh // TILE
        nslot = (nt + 1) // 2
        scale = hd ** -0.5 * math.log2(math.e)
        dma = pltpu.SemaphoreType.DMA
        return pl.pallas_call(
            functools.partial(kernel, ny, nx, nt, scale),
            out_shape=jax.ShapeDtypeStruct(q.shape, q.dtype),
            in_specs=[pl.BlockSpec(memory_space=pl.ANY)] * 3,
            out_specs=pl.BlockSpec(memory_space=pl.ANY),
            scratch_shapes=[
                pltpu.VMEM((nt, 3, rows, TILE, hd), BF16),
                pltpu.VMEM((2, 3, rows * TILE, hd), F32),
                pltpu.VMEM((nt, nx, 2, 3, 2, c2, hd), BF16),
                pltpu.VMEM((nt, nx, 2, 3, 2, c2, hd), BF16),
                pltpu.VMEM((nslot, 2, ny, nx, 3, 2, c2, hd), BF16),
                pltpu.VMEM((4 * ny + 2, nx * c2, 2 * nx * c2), F32),
                pltpu.VMEM((2, nx * c2, 2 * nx * c2), F32),
                pltpu.VMEM((nslot, ny, nx, 2, c2, hd), BF16),
                pltpu.VMEM((nt, TILE, 2, c2, hd), BF16),
                pltpu.VMEM((rows * TILE, hd), F32),
                pltpu.VMEM((nt, rows, TILE, hd), BF16),
                dma((nt, 3)), dma((nt, nx)), dma((nt, nx)), dma((nt, nx, 2)), dma((nslot, ny, nx)), dma((ny, nx)),
                dma((nslot, ny, nx)), dma((nslot, ny, nx)), dma((nslot, ny, nx)), dma((nt, TILE)), dma((nt,)),
            ],
            compiler_params=pltpu.CompilerParams(collective_id=0, has_side_effects=True, vmem_limit_bytes=56 * 1024 * 1024),
        )(q, k, v)

    return jax.shard_map(local, mesh=mesh, in_specs=(spec, spec, spec), out_specs=spec, check_vma=False)
```

time: 103 us -> 81.2 us (0.79)
  the two profiles are of different devices: /device:TPU:97 before, /device:TPU:120 now
where the time goes in v3:
time: 81.2 us; the launch traced here: 81.1 us
  Pallas kernels  78.6 us (97%)
  local copies, waits for them, and re-layouts  2.49 us (3%)
    pallas_call x1, Pallas kernels, local(): pl.pallas_call(functools.partial(kernel, ny, nx, nt, scale), out_shape=ja...  78.6 us
    unnamed x1, local copies, waits for them, and re-layouts  2.49 us

profile of v3, /device:TPU:120, one launch (start us, length us, event | category | flops | bytes accessed | tf_op | source)
XLA Modules:
  0.0 81.1 jit_solution(11863292256697438056)
XLA Ops:
  0.0 78.6 %shard_map.37 = bf16[128,40,128]{2,1,0:T(8,128)(2,1)} custom-call(bf16[128,40,128]{2,1,0:T(8,128)(2,1)} %q_hbm.1, bf16[128,40,128]{2,1,0:T(8,128)(2,1)} %k_hbm.1, bf16[128,40,128]{2,1,0:T(8,128)(2,1)} %v_hbm.1), custom_call_target="tpu_custom_call" | custom-call | tf_op jit(solution)/shard_map/pallas_call | solution.py:439
  78.6 2.5 %copy.5 = bf16[128,40,128]{2,1,0:T(8,128)(2,1)} copy(bf16[128,40,128]{2,1,0:T(8,128)(2,1)} %shard_map.37) | data formatting | bytes 2621440

commit v4 on v3

--- a/solution.py
+++ b/solution.py
@@ -333,10 +333,10 @@
         @pl.when(n == 0)
         def _():
             relay_two(1, 1)
+
+        @pl.when(n == 1)
+        def _():
             relay_two(1, 2)
-
-        @pl.when(n == 1)
-        def _():
             relay_two(1, 3)
 
         @pl.when((n == 1) | (n == 1 + pairs))

time: 81.2 us -> 80.4 us (level)
  the two profiles are of different devices: /device:TPU:120 before, /device:TPU:97 now
where the time goes in v4:
time: 80.4 us; the launch traced here: 78.9 us
  Pallas kernels  76.4 us (95%)
  local copies, waits for them, and re-layouts  2.49 us (3%)
    pallas_call x1, Pallas kernels, local(): pl.pallas_call(functools.partial(kernel, ny, nx, nt, scale), out_shape=ja...  76.4 us
    unnamed x1, local copies, waits for them, and re-layouts  2.49 us

profile of v4, /device:TPU:97, one launch (start us, length us, event | category | flops | bytes accessed | tf_op | source)
XLA Modules:
  0.0 78.9 jit_solution(17913145929271855134)
XLA Ops:
  0.0 76.4 %shard_map.37 = bf16[128,40,128]{2,1,0:T(8,128)(2,1)} custom-call(bf16[128,40,128]{2,1,0:T(8,128)(2,1)} %q_hbm.1, bf16[128,40,128]{2,1,0:T(8,128)(2,1)} %k_hbm.1, bf16[128,40,128]{2,1,0:T(8,128)(2,1)} %v_hbm.1), custom_call_target="tpu_custom_call" | custom-call | tf_op jit(solution)/shard_map/pallas_call | solution.py:439
  76.4 2.5 %copy.5 = bf16[128,40,128]{2,1,0:T(8,128)(2,1)} copy(bf16[128,40,128]{2,1,0:T(8,128)(2,1)} %shard_map.37) | data formatting | bytes 2621440

commit v5 on v4

--- a/solution.py
+++ b/solution.py
@@ -285,6 +285,8 @@
             l, acc = total[i]
             o = acc / jnp.sum(l, axis=-1, keepdims=True)
             ostage[slot, y, :, half] = o.astype(BF16).reshape(nx, c2, hd)
+            if y not in [t[0] for t in tiles[i + 1:]]:
+                send_back(slot, y)
 
     def send_back(slot, y):
         def back(sx_, _):
@@ -350,8 +352,6 @@
                 arrived(slot)
 
         attend(slot, pair)
-        send_back(slot, 2 * pair)
-        send_back(slot, 2 * pair + 1)
         return 0
 
     lax.fori_loop(0, 1 + nslot * ny // 2, step, 0)

time: 80.4 us -> 83.2 us (1.035); the launches traced: 78.9 us -> 83.1 us
  Pallas kernels: 76.4 us -> 80.6 us
    pallas_call x1, Pallas kernels: 76.4 us -> 80.6 us  [local(): pl.pallas_call(functools.partial(kernel, ny, nx, nt, scale), out_shape=ja...]
where the time goes in v5:
time: 83.2 us; the launch traced here: 83.1 us
  Pallas kernels  80.6 us (97%)
  local copies, waits for them, and re-layouts  2.49 us (3%)
    pallas_call x1, Pallas kernels, local(): pl.pallas_call(functools.partial(kernel, ny, nx, nt, scale), out_shape=ja...  80.6 us
    unnamed x1, local copies, waits for them, and re-layouts  2.49 us

profile of v5, /device:TPU:97, one launch (start us, length us, event | category | flops | bytes accessed | tf_op | source)
XLA Modules:
  0.0 83.1 jit_solution(2302083323178201352)
XLA Ops:
  0.0 80.6 %shard_map.37 = bf16[128,40,128]{2,1,0:T(8,128)(2,1)} custom-call(bf16[128,40,128]{2,1,0:T(8,128)(2,1)} %q_hbm.1, bf16[128,40,128]{2,1,0:T(8,128)(2,1)} %k_hbm.1, bf16[128,40,128]{2,1,0:T(8,128)(2,1)} %v_hbm.1), custom_call_target="tpu_custom_call" | custom-call | tf_op jit(solution)/shard_map/pallas_call | solution.py:439
  80.6 2.5 %copy.5 = bf16[128,40,128]{2,1,0:T(8,128)(2,1)} copy(bf16[128,40,128]{2,1,0:T(8,128)(2,1)} %shard_map.37) | data formatting | bytes 2621440
